TPU v7x, 512 devices: a whole 4x8x8 slice. The times are simulated.
512 devices in a mesh: gx: 64 (over y, z_lo, core), gy: 8 (over x, z_hi).
Axes of the slice: x: 4, y: 8, z: 8 (z_hi: 2, z_lo: 4; z = z_hi * 4 + z_lo), core: 2. Of those that a mesh axis runs over, the one named last changes fastest.
Arguments:
- fluid_velocity: float32 [3, 256, 128, 128], P(None, 'gx', 'gy'), may hold values from -6 to 6
- particle_velocity: float32 [64, 8, 4, 3, 128], P('gx', 'gy'), may hold values from -6 to 6
- particle_volume: float32 [64, 8, 4, 128], P('gx', 'gy'), may hold values from 0.02 to 0.3
- satellite_cells: int32 [64, 8, 4, 29, 128], P('gx', 'gy'), may hold values from 0 to 13823
- live_blocks: int32 [64, 8], P('gx', 'gy'), may hold values from 1 to 4
Outputs:
- void_fraction: float32 [256, 128, 128], P('gx', 'gy')
- drag: float32 [64, 8, 4, 3, 128], P('gx', 'gy')
Inputs may be any that keep to these rules, and one draw needn't show every extreme that they name: `live_blocks`: blocks from this number on hold no live particles.
All inputs are finite; a program needn't handle non-finite values.
Results may differ from a plain program's by a relative error of at most 0.00029.
Values sent between devices are 32-bit elements; how exact they have to be, the bound alone decides.
No kernel may reach another device: no remote copies, remote signals or barrier semaphores. Data moves between devices by JAX's collectives and lax.ppermute only.
A program may use at most 64 MiB of HBM per device.

v0:
```python
import math

import jax
import jax.numpy as jnp
from jax import lax
from jax.sharding import PartitionSpec as P

exponent = -2.65
drag_scale = 2.0
void_floor = 0.1


def passed_along(value, axis, steps):
    count = lax.axis_size(axis)
    pairs = [(source, (source + steps) % count) for source in range(count)]
    return lax.ppermute(value, axis, pairs)


def padded(cells, sides, width):
    for axis, dim in sides:
        count = lax.axis_size(axis)
        head = lax.slice_in_dim(cells, 0, width, axis=dim)
        tail = lax.slice_in_dim(cells, cells.shape[dim] - width, cells.shape[dim], axis=dim)
        cells = jnp.concatenate(
            [
                lax.ppermute(tail, axis, [(i, (i + 1) % count) for i in range(count)]),
                cells,
                lax.ppermute(head, axis, [((i + 1) % count, i) for i in range(count)]),
            ],
            axis=dim,
        )
    return cells


def body(fluid_velocity, particle_velocity, particle_volume, satellite_cells, live_blocks):
    cells_x = fluid_velocity.shape[1]
    cells_y = fluid_velocity.shape[2]
    cells_z = fluid_velocity.shape[3]
    wide_x = cells_x + 2
    wide_y = cells_y + 2
    satellites = satellite_cells[0, 0]
    volume = particle_volume[0, 0]
    velocity = particle_velocity[0, 0]
    live_count = live_blocks[0, 0]
    block_count = satellites.shape[0]
    point_count = satellites.shape[1]
    lane_count = satellites.shape[2]
    group_size = math.gcd(block_count, 8)
    turns = (live_count + group_size - 1) // group_size

    def group_share(group_index):
        start = group_index * group_size
        alive = (start + jnp.arange(group_size, dtype=jnp.int32) < live_count).astype(jnp.float32)
        return volume * alive[:, None] / point_count

    def deposit(group_index, deposit_tile):
        start = group_index * group_size
        weights = jnp.broadcast_to(group_share(group_index)[:, None, :], satellites.shape)
        return deposit_tile.at[satellites.reshape(-1)].add(weights.reshape(-1))

    empty_tile = jnp.zeros((wide_x * wide_y * cells_z,), jnp.float32)
    deposit_tile = lax.fori_loop(0, turns, deposit, empty_tile).reshape(wide_x, wide_y, cells_z)
    below_x = passed_along(deposit_tile[-1], "gx", 1)
    above_x = passed_along(deposit_tile[0], "gx", -1)
    interior = deposit_tile[1:-1].at[0].add(below_x).at[-1].add(above_x)
    below_y = passed_along(interior[:, -1], "gy", 1)
    above_y = passed_along(interior[:, 0], "gy", -1)
    solid_volume = interior[:, 1:-1].at[:, 0].add(below_y).at[:, -1].add(above_y)
    void_fraction = jnp.maximum(1.0 - solid_volume, void_floor)
    stacked = jnp.concatenate([fluid_velocity, void_fraction[None]], axis=0)
    fields_wide = padded(stacked, (("gx", 1), ("gy", 2)), 1)
    velocity_wide = fields_wide[:3]
    void_wide = fields_wide[3]
    resistance = (void_wide**exponent).reshape(-1)
    flow = velocity_wide.reshape(3, -1)

    def drag_group(group_index, drag_out):
        start = group_index * group_size
        volume_share = group_share(group_index)
        weight_at = jnp.take(resistance, satellites)
        flow_at = jnp.take(flow, satellites, axis=1)
        weight_sum = jnp.sum(weight_at, axis=1)
        pulling = jnp.transpose(jnp.sum(weight_at[None] * flow_at, axis=2), (1, 0, 2))
        force = (
            drag_scale * volume_share[:, None, :] * (pulling - velocity * weight_sum[:, None, :])
        )
        return force

    empty_drag = jnp.zeros((block_count, 3, lane_count), jnp.float32)
    drag_out = lax.fori_loop(0, turns, drag_group, empty_drag)
    return (void_fraction, drag_out[None, None])


def solution(mesh):
    placed = (
        P(None, "gx", "gy", None),
        P("gx", "gy", None, None, None),
        P("gx", "gy", None, None),
        P("gx", "gy", None, None, None),
        P("gx", "gy"),
    )
    return jax.shard_map(
        body,
        mesh=mesh,
        in_specs=placed,
        out_specs=(P("gx", "gy", None), P("gx", "gy", None, None, None)),
        check_vma=False,
    )
```

profile of v0, /device:TPU:6, one launch (start us, length us, event | category | flops | bytes accessed | tf_op | source)
XLA Modules:
  0.0 262.7 jit_solution(17241127977198463528)
XLA Ops:
  1.3 0.8 copy.21
  2.1 0.1 reshape_squeeze.3
  2.2 0.5 copy-done.1
  2.8 82.6 %while.29 = (s32[]{:T(128)}, f32[13824]{0:T(1024)S(1)}, s32[]{:T(128)}, s32[1,1,4,29,128]{4,3,2,1,0:T(8,128)}, s32[]{:T(128)}, /*index=5*/f32[4,128]{1,0:T(4,128)}, s32[14848,1]{0,1:T(1,128)S(1)}, s32[]{:T(128)}, s32[]{:T(128)}) while((s32[]{:T(128)}, f32[13824]{0:T(1024)S(1)}, s32[]{:T(128)}, s32[1,1,4,29,128]{4,3,2,1,0:T(8,128)}, ...), condition=%wide.wide.region_2.3_spmd, body=%wide.wide.region_0.2_spmd.sunk | while | flops 60431 | bytes 540817 | solution.py:62
  2.8 0.7 compare_convert_fusion.6
  3.5 0.8 multiply_multiply_fusion.6
  4.2 0.2 fusion.13
  4.4 80.9 %scatter_fusion = f32[13824]{0:T(1024)S(1)} fusion(f32[13824]{0:T(1024)S(1)} %get-tuple-element.434, s32[14848]{0:T(1024)S(1)} %fusion.13, f32[14848]{0:T(1024)S(1)} %reshape.357), kind=kCustom, calls=%fused_computation.2.clone.clone.1 | custom fusion | flops 14848 | bytes 237568 | tf_op jit(solution)/shard_map/while/body/scatter-add | solution.py:59
  85.4 1.9 collective-permute-start
  87.3 9.3 %collective-permute-start.1 = (f32[18,128]{1,0:T(8,128)S(1)}, f32[18,128]{1,0:T(8,128)S(1)}, u32[]{:S(2)}, u32[]{:S(2)}) collective-permute-start(f32[18,128]{1,0:T(8,128)S(1)} %get-tuple-element.300), channel_id=1, source_target_pairs={{0,504},{8,0},{16,8},{24,16},{32,24},{40,32},{48,40},{56,48},{64,5... | collective-permute-start | bytes 27656 | tf_op jit(solution)/shard_map/ppermute | solution.py:16
  96.7 1.3 collective-permute-done.1
  98.0 8.4 %collective-permute-start.2 = (f32[4,128]{1,0:T(4,128)S(1)}, f32[4,128]{1,0:T(4,128)S(1)}, u32[]{:S(2)}, u32[]{:S(2)}) collective-permute-start(f32[4,128]{1,0:T(4,128)S(1)} %bitcast.56), channel_id=1, source_target_pairs={{0,1},{1,2},{2,3},{3,4},{4,5},{5,6},{6,7},{7,0},{8,9},{9,10},{10,1... | collective-permute-start | bytes 6152 | tf_op jit(solution)/shard_map/ppermute | solution.py:16
  106.5 3.0 %collective-permute-start.3 = (f32[4,128]{1,0:T(4,128)S(1)}, f32[4,128]{1,0:T(4,128)S(1)}, u32[]{:S(2)}, u32[]{:S(2)}) collective-permute-start(f32[4,128]{1,0:T(4,128)S(1)} %bitcast.55), channel_id=1, source_target_pairs={{0,7},{1,0},{2,1},{3,2},{4,3},{5,4},{6,5},{7,6},{8,15},{9,8},{10,9... | collective-permute-start | bytes 6152 | tf_op jit(solution)/shard_map/ppermute | solution.py:16
  109.6 6.3 %collective-permute-done.3 = f32[4,128]{1,0:T(4,128)S(1)} collective-permute-done((f32[4,128]{1,0:T(4,128)S(1)}, f32[4,128]{1,0:T(4,128)S(1)}, u32[]{:S(2)}, u32[]{:S(2)}) %collective-permute-start.3) | collective-permute-done | bytes 2080 | tf_op jit(solution)/shard_map/ppermute | solution.py:16
  116.0 1.9 collective-permute-start.4
  117.9 7.5 %collective-permute-start.5 = (f32[4,1,16,128]{3,2,1,0:T(8,128)S(1)}, f32[4,1,16,128]{3,2,1,0:T(8,128)S(1)}, u32[]{:S(2)}, u32[]{:S(2)}) collective-permute-start(f32[4,1,16,128]{3,2,1,0:T(8,128)S(1)} %get-tuple-element.299), channel_id=1, source_target_pairs={{8,0},{16,8},{24,16},{32,24},{40,32},{48,40},{56,48},{64,56},{72,6... | collective-permute-start | bytes 98312 | tf_op jit(solution)/shard_map/ppermute | solution.py:28
  125.5 1.5 collective-permute-done.5
  127.1 5.5 %collective-permute-start.6 = (f32[4,6,1,128]{3,2,1,0:T(1,128)S(1)}, f32[4,6,1,128]{3,2,1,0:T(1,128)S(1)}, u32[]{:S(2)}, u32[]{:S(2)}) collective-permute-start(f32[4,6,1,128]{3,2,1,0:T(1,128)S(1)} %get-tuple-element.296), channel_id=1, source_target_pairs={{0,1},{1,2},{2,3},{3,4},{4,5},{5,6},{6,7},{7,0},{8,9},{9,10},{10,1... | collective-permute-start | bytes 36872 | tf_op jit(solution)/shard_map/ppermute | solution.py:26
  132.6 5.1 %collective-permute-start.7 = (f32[4,6,1,128]{3,2,1,0:T(1,128)S(1)}, f32[4,6,1,128]{3,2,1,0:T(1,128)S(1)}, u32[]{:S(2)}, u32[]{:S(2)}) collective-permute-start(f32[4,6,1,128]{3,2,1,0:T(1,128)S(1)} %get-tuple-element.297), channel_id=1, source_target_pairs={{1,0},{2,1},{3,2},{4,3},{5,4},{6,5},{7,6},{0,7},{9,8},{10,9},{11,1... | collective-permute-start | bytes 36872 | tf_op jit(solution)/shard_map/ppermute | solution.py:28
  137.7 0.6 copy.30
  138.4 3.7 %collective-permute-done.7 = f32[4,6,1,128]{3,2,1,0:T(1,128)S(1)} collective-permute-done((f32[4,6,1,128]{3,2,1,0:T(1,128)S(1)}, f32[4,6,1,128]{3,2,1,0:T(1,128)S(1)}, u32[]{:S(2)}, u32[]{:S(2)}) %collective-permute-start.7) | collective-permute-done | bytes 12320 | tf_op jit(solution)/shard_map/ppermute | solution.py:28
  142.1 0.1 maximum_power_fusion
  142.2 76.4 %gather_fusion = f32[14848]{0:T(1024)S(1)} fusion(f32[13824]{0:T(1024)S(1)} %pow.12, s32[15360]{0:T(1024)S(1)} %pad_clamp_fusion), kind=kCustom, calls=%fused_computation | custom fusion | bytes 178176 | tf_op jit(solution)/shard_map/while/body/jit(_take)/gather | solution.py:80
  218.7 4.3 %copy.28 = f32[3,6,18,128]{0,3,2,1:T(8,128)} copy(f32[3,6,18,128]{3,2,1,0:T(8,128)S(1)} %pad_maximum_fusion) | data formatting | bytes 331776 | tf_op jit(solution)/shard_map/slice | solution.py:72
  223.1 31.1 %gather_fusion.1 = f32[14848,3]{1,0:T(8,128)} fusion(f32[3,13824]{0,1:T(8,128)} %bitcast.48, s32[15360]{0:T(1024)S(1)} %pad_clamp_fusion), kind=kCustom, calls=%fused_computation.1 | custom fusion | bytes 415744 | tf_op jit(solution)/shard_map/while/body/jit(_take)/gather | solution.py:81
  254.1 6.5 %multiply_reduce_fusion = f32[4,128,3]{2,1,0:T(8,128)S(1)} fusion(f32[4,29,128,3]{3,2,1,0:T(8,128)} %bitcast.49, f32[4,29,128]{2,1,0:T(8,128)S(1)} %get-tuple-element.294, pred[4,29,128]{2,1,0:T(8,128)(4,1)S(1)} %get-tuple-element.295), kind=kLoop, calls=%fused_computation.11 | loop fusion | flops 132096 | bytes 258560 | tf_op jit(solution)/shard_map/while/body/reduce_sum | solution.py:83
  260.6 0.1 copy.29
  260.7 0.6 broadcast_in_dim.50
  261.3 1.3 while.28
  261.3 0.6 compare_convert_fusion.5
  262.0 0.1 multiply_multiply_fusion.5
  262.1 0.6 fusion.12
  (39 shorter events, 0.3 us)
Async XLA Ops:
  2.1 0.6 copy-start.1
  2.7 103.7 %copy-start.4 = (f32[3,4,16,128]{3,2,1,0:T(8,128)S(1)}, f32[3,4,16,128]{3,2,1,0:T(8,128)}, u32[]{:S(2)}) copy-start(f32[3,4,16,128]{3,2,1,0:T(8,128)} %param.17) | copy-start | bytes 294916
  2.8 122.7 %copy-start = (s32[1,1,4,29,128]{4,2,3,1,0:T(4,128)S(1)}, s32[1,1,4,29,128]{4,2,3,1,0:T(4,128)}, u32[]{:S(2)}) copy-start(s32[1,1,4,29,128]{4,2,3,1,0:T(4,128)} %param.20) | copy-start | bytes 178180
  85.4 11.3 %collective-permute-start = (f32[18,128]{1,0:T(8,128)S(1)}, f32[18,128]{1,0:T(8,128)S(1)}, u32[]{:S(2)}, u32[]{:S(2)}) collective-permute-start(f32[18,128]{1,0:T(8,128)S(1)} %get-tuple-element.301), channel_id=1, source_target_pairs={{0,8},{8,16},{16,24},{24,32},{32,40},{40,48},{48,56},{56,64},{64,7... | collective-permute-start | bytes 27656 | tf_op jit(solution)/shard_map/ppermute | solution.py:16
  87.3 10.7 %collective-permute-start.1 = (f32[18,128]{1,0:T(8,128)S(1)}, f32[18,128]{1,0:T(8,128)S(1)}, u32[]{:S(2)}, u32[]{:S(2)}) collective-permute-start(f32[18,128]{1,0:T(8,128)S(1)} %get-tuple-element.300), channel_id=1, source_target_pairs={{0,504},{8,0},{16,8},{24,16},{32,24},{40,32},{48,40},{56,48},{64,5... | collective-permute-start | bytes 27656 | tf_op jit(solution)/shard_map/ppermute | solution.py:16
  98.0 11.5 %collective-permute-start.2 = (f32[4,128]{1,0:T(4,128)S(1)}, f32[4,128]{1,0:T(4,128)S(1)}, u32[]{:S(2)}, u32[]{:S(2)}) collective-permute-start(f32[4,128]{1,0:T(4,128)S(1)} %bitcast.56), channel_id=1, source_target_pairs={{0,1},{1,2},{2,3},{3,4},{4,5},{5,6},{6,7},{7,0},{8,9},{9,10},{10,1... | collective-permute-start | bytes 6152 | tf_op jit(solution)/shard_map/ppermute | solution.py:16
  106.5 9.4 %collective-permute-start.3 = (f32[4,128]{1,0:T(4,128)S(1)}, f32[4,128]{1,0:T(4,128)S(1)}, u32[]{:S(2)}, u32[]{:S(2)}) collective-permute-start(f32[4,128]{1,0:T(4,128)S(1)} %bitcast.55), channel_id=1, source_target_pairs={{0,7},{1,0},{2,1},{3,2},{4,3},{5,4},{6,5},{7,6},{8,15},{9,8},{10,9... | collective-permute-start | bytes 6152 | tf_op jit(solution)/shard_map/ppermute | solution.py:16
  116.0 9.6 %collective-permute-start.4 = (f32[4,1,16,128]{3,2,1,0:T(8,128)S(1)}, f32[4,1,16,128]{3,2,1,0:T(8,128)S(1)}, u32[]{:S(2)}, u32[]{:S(2)}) collective-permute-start(f32[4,1,16,128]{3,2,1,0:T(8,128)S(1)} %get-tuple-element.298), channel_id=1, source_target_pairs={{0,8},{8,16},{16,24},{24,32},{32,40},{40,48},{48,56},{56,64},{64,7... | collective-permute-start | bytes 98312 | tf_op jit(solution)/shard_map/ppermute | solution.py:26
  117.9 9.1 %collective-permute-start.5 = (f32[4,1,16,128]{3,2,1,0:T(8,128)S(1)}, f32[4,1,16,128]{3,2,1,0:T(8,128)S(1)}, u32[]{:S(2)}, u32[]{:S(2)}) collective-permute-start(f32[4,1,16,128]{3,2,1,0:T(8,128)S(1)} %get-tuple-element.299), channel_id=1, source_target_pairs={{8,0},{16,8},{24,16},{32,24},{40,32},{48,40},{56,48},{64,56},{72,6... | collective-permute-start | bytes 98312 | tf_op jit(solution)/shard_map/ppermute | solution.py:28
  127.1 11.3 %collective-permute-start.6 = (f32[4,6,1,128]{3,2,1,0:T(1,128)S(1)}, f32[4,6,1,128]{3,2,1,0:T(1,128)S(1)}, u32[]{:S(2)}, u32[]{:S(2)}) collective-permute-start(f32[4,6,1,128]{3,2,1,0:T(1,128)S(1)} %get-tuple-element.296), channel_id=1, source_target_pairs={{0,1},{1,2},{2,3},{3,4},{4,5},{5,6},{6,7},{7,0},{8,9},{9,10},{10,1... | collective-permute-start | bytes 36872 | tf_op jit(solution)/shard_map/ppermute | solution.py:26
  132.6 9.5 %collective-permute-start.7 = (f32[4,6,1,128]{3,2,1,0:T(1,128)S(1)}, f32[4,6,1,128]{3,2,1,0:T(1,128)S(1)}, u32[]{:S(2)}, u32[]{:S(2)}) collective-permute-start(f32[4,6,1,128]{3,2,1,0:T(1,128)S(1)} %get-tuple-element.297), channel_id=1, source_target_pairs={{1,0},{2,1},{3,2},{4,3},{5,4},{6,5},{7,6},{0,7},{9,8},{10,9},{11,1... | collective-permute-start | bytes 36872 | tf_op jit(solution)/shard_map/ppermute | solution.py:28
  218.7 42.7 %copy-start.2 = (f32[4,128]{1,0:T(4,128)S(1)}, f32[4,128]{1,0:T(4,128)}, u32[]{:S(2)}) copy-start(f32[4,128]{1,0:T(4,128)} %get-tuple-element.483) | copy-start | bytes 6148
  218.7 42.6 %copy-start.3 = (f32[1,1,4,3,128]{4,2,3,1,0:T(4,128)S(1)}, f32[1,1,4,3,128]{4,2,3,1,0:T(4,128)}, u32[]{:S(2)}) copy-start(f32[1,1,4,3,128]{4,2,3,1,0:T(4,128)} %param.18) | copy-start | bytes 18436
where the time goes:
time: 264 us; the launch traced here: 263 us
  local copies, waits for them, and re-layouts  115 us (44%)
  other arithmetic  90.6 us (34%)
  starting transfers between devices  42.8 us (16%)
  waiting for transfers between devices  12.9 us (5%)
    scatter-add x1, other arithmetic, deposit(): return deposit_tile.at[satellites.reshape(-1)].add(weights.reshape(-1))  80.9 us
    gather x2, local copies, waits for them, and re-layouts, drag_group(): weight_at = jnp.take(resistance, satellites)  76.4 us
    gather x1, local copies, waits for them, and re-layouts, drag_group(): flow_at = jnp.take(flow, satellites, axis=1)  31.1 us
    ppermute x4, starting transfers between devices, passed_along(): return lax.ppermute(value, axis, pairs)  22.7 us
    ppermute x2, starting transfers between devices, padded(): lax.ppermute(head, axis, [((i + 1) % count, i) for i in range(count)])  12.7 us
    ppermute x4, waiting for transfers between devices, passed_along(): return lax.ppermute(value, axis, pairs)  7.66 us
    ppermute x2, starting transfers between devices, padded(): lax.ppermute(tail, axis, [(i, (i + 1) % count) for i in range(count)])  7.47 us
    reduce_sum x1, other arithmetic, drag_group(): jnp.sum(weight_at[None] * flow_at, axis=2)  6.51 us
  transfers between devices with their start and end apart: 8, of which 4 were waited for; matrix products, arithmetic and copies ran while one was open for 0% of the time, Pallas kernels for 0%

commit v1 on v0

v1 whole, which is shorter than its diff:
```python
import functools

import jax
import jax.numpy as jnp
from jax import lax
from jax.experimental import pallas as pl
from jax.experimental.pallas import tpu as pltpu
from jax.sharding import PartitionSpec as P

exponent = -2.65
drag_scale = 2.0
void_floor = 0.1

cells_x, cells_y, cells_z = 4, 16, 128
wide_y = cells_y + 2
inner_rows = cells_x * cells_y
x_low, x_high = inner_rows, inner_rows + cells_y
y_low, y_high = inner_rows + 2 * cells_y, inner_rows + 2 * cells_y + 8
tile_rows = y_high + 8
x_rows, y_rows = 88, 40


def split_cells(cells):
    lane = cells & (cells_z - 1)
    column = cells >> 7
    i = (column * 3641) >> 16
    j = column - i * wide_y
    inner = (i - 1) * cells_y + (j - 1)
    row = jnp.where(i == 0, x_low + j - 1, jnp.where(i == cells_x + 1, x_high + j - 1, inner))
    row = jnp.where(j == 0, y_low + i, jnp.where(j == cells_y + 1, y_high + i, row))
    return row, lane


def shares(live, volume, block, points):
    alive = jnp.where(block < live, 1.0, 0.0)
    return volume[block : block + 1] * alive / points


def halves(value):
    high = value.astype(jnp.bfloat16)
    low = (value - high.astype(jnp.float32)).astype(jnp.bfloat16)
    return high, low


def points_of(blocks, points):
    every = [(b, s) for b in range(blocks) for s in range(points)]
    return [every[at : at + 2] for at in range(0, len(every), 2)]


def deposit_kernel(live_ref, cells_ref, volume_ref, velocity_ref, tile_ref, up_ref, down_ref):
    blocks, points = cells_ref.shape[0], cells_ref.shape[1]
    live = live_ref[0, 0]
    volume = volume_ref[...]
    row_at = lax.broadcasted_iota(jnp.int32, (tile_rows, 128), 0).astype(jnp.float32).astype(jnp.bfloat16)
    lane_at = lax.broadcasted_iota(jnp.int32, (cells_z, 128), 0).astype(jnp.float32).astype(jnp.bfloat16)
    rows, lanes, high, low = [], [], [], []
    for b in range(blocks):
        row, lane = split_cells(cells_ref[b])
        rows.append(row.astype(jnp.float32).astype(jnp.bfloat16))
        lanes.append(lane.astype(jnp.float32).astype(jnp.bfloat16))
        h, l = halves(shares(live, volume, b, points))
        high.append(h)
        low.append(l)
    one = jnp.ones((), jnp.bfloat16)
    zero = jnp.zeros((), jnp.bfloat16)
    total = jnp.zeros((tile_rows, 2 * cells_z), jnp.float32)
    for pair in points_of(blocks, points):
        left, right = [], []
        for b, s in pair:
            left.append(jnp.where(row_at == rows[b][s : s + 1], one, zero))
            at_lane = lane_at == lanes[b][s : s + 1]
            right.append(
                jnp.concatenate([jnp.where(at_lane, high[b], zero), jnp.where(at_lane, low[b], zero)], axis=0)
            )
        total += lax.dot_general(
            jnp.concatenate(left, axis=1),
            jnp.concatenate(right, axis=1),
            (((1,), (1,)), ((), ())),
            preferred_element_type=jnp.float32,
        )
    tile_ref[...] = total[:, :cells_z] + total[:, cells_z:]

    def fill(out_ref, edge, beyond, layers, velocity_layer):
        first = (layers[0] - 1) * cells_y if 1 <= layers[0] <= cells_x else edge
        second = (layers[1] - 1) * cells_y if 1 <= layers[1] <= cells_x else edge
        out_ref[0:16] = tile_ref[first : first + 16]
        out_ref[16:32] = tile_ref[second : second + 16]
        out_ref[32:40] = jnp.zeros((8, 128), jnp.float32)
        out_ref[32:34] = tile_ref[y_low + layers[0] : y_low + layers[0] + 2]
        out_ref[34:36] = tile_ref[y_high + layers[0] : y_high + layers[0] + 2]
        for f in range(3):
            out_ref[40 + 16 * f : 56 + 16 * f] = velocity_ref[f, velocity_layer]

    fill(up_ref, x_high, None, (cells_x, cells_x + 1), cells_x - 1)
    fill(down_ref, x_low, None, (0, 1), 0)


def middle_kernel(tile_ref, velocity_ref, below_ref, above_ref, out_ref, up_ref, down_ref):
    out_ref[...] = tile_ref[...]
    out_ref[x_low : x_low + 16] += below_ref[0:16]
    out_ref[0:16] += below_ref[16:32]
    out_ref[y_low : y_low + 2] += below_ref[32:34]
    out_ref[y_high : y_high + 2] += below_ref[34:36]
    last = inner_rows - 16
    out_ref[last : last + 16] += above_ref[0:16]
    out_ref[x_high : x_high + 16] += above_ref[16:32]
    out_ref[y_low + 4 : y_low + 6] += above_ref[32:34]
    out_ref[y_high + 4 : y_high + 6] += above_ref[34:36]

    def fill(dest_ref, near, halo, order):
        dest_ref[...] = jnp.zeros((y_rows, 128), jnp.float32)
        at = 8 * order[0]
        dest_ref[at : at + 1] = out_ref[x_low + near : x_low + near + 1]
        for i in range(cells_x):
            dest_ref[at + 1 + i : at + 2 + i] = out_ref[16 * i + near : 16 * i + near + 1]
        dest_ref[at + 5 : at + 6] = out_ref[x_high + near : x_high + near + 1]
        at = 8 * order[1]
        dest_ref[at : at + 6] = out_ref[halo : halo + 6]
        for f in range(3):
            at = 16 + 8 * f
            dest_ref[at : at + 1] = below_ref[40 + 16 * f + near : 41 + 16 * f + near]
            for i in range(cells_x):
                dest_ref[at + 1 + i : at + 2 + i] = velocity_ref[f, i, near : near + 1]
            dest_ref[at + 5 : at + 6] = above_ref[40 + 16 * f + near : 41 + 16 * f + near]

    fill(up_ref, cells_y - 1, y_high, (0, 1))
    fill(down_ref, 0, y_low, (0, 1))


def drag_kernel(
    live_ref,
    cells_ref,
    volume_ref,
    particle_ref,
    velocity_ref,
    tile_ref,
    x_below_ref,
    x_above_ref,
    y_below_ref,
    y_above_ref,
    void_ref,
    drag_ref,
    solid_ref,
):
    blocks, points = cells_ref.shape[0], cells_ref.shape[1]
    live = live_ref[0, 0]
    volume = volume_ref[...]
    solid_ref[...] = tile_ref[...]

    def take_in(source_ref, near, halo):
        solid_ref[halo : halo + 6] += source_ref[0:6]
        solid_ref[x_low + near : x_low + near + 1] += source_ref[8:9]
        for i in range(cells_x):
            solid_ref[16 * i + near : 16 * i + near + 1] += source_ref[9 + i : 10 + i]
        solid_ref[x_high + near : x_high + near + 1] += source_ref[13:14]

    take_in(y_below_ref, 0, y_low)
    take_in(y_above_ref, cells_y - 1, y_high)
    void = jnp.maximum(1.0 - solid_ref[...], void_floor)
    for i in range(cells_x):
        void_ref[i] = void[16 * i : 16 * i + 16]
    resistance = jnp.exp(exponent * jnp.log(void))
    fields = [resistance]
    for f in range(3):
        flow = jnp.concatenate(
            [velocity_ref[f, i] for i in range(cells_x)]
            + [
                x_below_ref[40 + 16 * f : 56 + 16 * f],
                x_above_ref[40 + 16 * f : 56 + 16 * f],
                y_below_ref[16 + 8 * f : 24 + 8 * f],
                y_above_ref[16 + 8 * f : 24 + 8 * f],
            ],
            axis=0,
        )
        fields.append(resistance * flow)
    table = jnp.concatenate(fields, axis=0)
    table = jnp.concatenate(list(halves(table)), axis=1)

    row_at = lax.broadcasted_iota(jnp.int32, (tile_rows, 128), 0)
    lane_at = lax.broadcasted_iota(jnp.int32, (cells_z, 128), 0).astype(jnp.float32).astype(jnp.bfloat16)
    one = jnp.ones((), jnp.bfloat16)
    zero = jnp.zeros((), jnp.bfloat16)
    rows, lanes = [], []
    for b in range(blocks):
        row, lane = split_cells(cells_ref[b])
        rows.append(row)
        lanes.append(lane.astype(jnp.float32).astype(jnp.bfloat16))
    sums = [[jnp.zeros((8, 128), jnp.float32) for _ in range(4)] for _ in range(blocks)]
    for pair in points_of(blocks, points):
        right = [jnp.where(lane_at == lanes[b][s : s + 1], one, zero) for b, s in pair]
        right = jnp.concatenate(right, axis=1)
        found = jnp.dot(table, jnp.concatenate([right, right], axis=0), preferred_element_type=jnp.float32)
        for n, (b, s) in enumerate(pair):
            at_row = row_at == rows[b][s : s + 1]
            for f in range(4):
                part = found[f * tile_rows : (f + 1) * tile_rows, n * 128 : n * 128 + 128]
                part = jnp.where(at_row, part, 0.0)
                sums[b][f] = sums[b][f] + jnp.sum(part.reshape(tile_rows // 8, 8, 128), axis=0)
    for b in range(blocks):
        share = shares(live, volume, b, points)
        weight = jnp.sum(sums[b][0], axis=0, keepdims=True)
        for f in range(3):
            pulling = jnp.sum(sums[b][f + 1], axis=0, keepdims=True)
            drag_ref[b, f : f + 1] = drag_scale * share * (pulling - particle_ref[b, f : f + 1] * weight)


def on_chip(count):
    return [pl.BlockSpec(memory_space=pltpu.VMEM)] * count


def rows_of(count):
    return jax.ShapeDtypeStruct((count, 128), jnp.float32)


def both_ways(up, down, axis):
    count = lax.axis_size(axis)
    below = lax.ppermute(up, axis, [(i, (i + 1) % count) for i in range(count)])
    above = lax.ppermute(down, axis, [((i + 1) % count, i) for i in range(count)])
    return below, above


def body(fluid_velocity, particle_velocity, particle_volume, satellite_cells, live_blocks):
    cells = satellite_cells[0, 0]
    volume = particle_volume[0, 0]
    particles = particle_velocity[0, 0]
    blocks = cells.shape[0]
    scalar = pl.BlockSpec(memory_space=pltpu.SMEM)
    tile, x_up, x_down = pl.pallas_call(
        deposit_kernel,
        out_shape=(rows_of(tile_rows), rows_of(x_rows), rows_of(x_rows)),
        in_specs=[scalar] + on_chip(3),
        out_specs=tuple(on_chip(3)),
        name="deposit",
    )(live_blocks, cells, volume, fluid_velocity)
    x_below, x_above = both_ways(x_up, x_down, "gx")
    tile, y_up, y_down = pl.pallas_call(
        middle_kernel,
        out_shape=(rows_of(tile_rows), rows_of(y_rows), rows_of(y_rows)),
        in_specs=on_chip(4),
        out_specs=tuple(on_chip(3)),
        name="middle",
    )(tile, fluid_velocity, x_below, x_above)
    y_below, y_above = both_ways(y_up, y_down, "gy")
    void, drag = pl.pallas_call(
        drag_kernel,
        out_shape=(
            jax.ShapeDtypeStruct((cells_x, cells_y, cells_z), jnp.float32),
            jax.ShapeDtypeStruct((blocks, 3, 128), jnp.float32),
        ),
        in_specs=[scalar] + on_chip(9),
        out_specs=tuple(on_chip(2)),
        scratch_shapes=[pltpu.VMEM((tile_rows, 128), jnp.float32)],
        name="drag",
    )(live_blocks, cells, volume, particles, fluid_velocity, tile, x_below, x_above, y_below, y_above)
    return void, drag[None, None]


def solution(mesh):
    placed = (
        P(None, "gx", "gy", None),
        P("gx", "gy", None, None, None),
        P("gx", "gy", None, None),
        P("gx", "gy", None, None, None),
        P("gx", "gy"),
    )
    return jax.shard_map(
        body,
        mesh=mesh,
        in_specs=placed,
        out_specs=(P("gx", "gy", None), P("gx", "gy", None, None, None)),
        check_vma=False,
    )
```

time: 264 us -> 49.1 us (0.19)
  local copies, waits for them, and re-layouts: 115 us -> 4.57 us
  other arithmetic: 90.6 us -> 0 us
  starting transfers between devices: 42.8 us -> 22.8 us
  Pallas kernels: 0 us -> 11.2 us
  waiting for transfers between devices: 12.9 us -> 8.75 us
    gather x3 -> x0, local copies, waits for them, and re-layouts: 107 us -> none  [the longest x2 76.4 us: drag_group(): weight_at = jnp.take(resistance, satellites)]
    scatter-add x5 -> x0, other arithmetic: 81 us -> none  [the longest x1 80.9 us: deposit(): return deposit_tile.at[satellites.reshape(-1)].add(weights.reshape(-1))]
    ppermute x8 -> x4, starting transfers between devices: 42.8 us -> 22.8 us  [the longest x2 12.7 us: both_ways(): lax.ppermute(down, axis, [((i + 1) % count, i) for i in range(count)])]
    pallas_call x0 -> x3, Pallas kernels: none -> 11.2 us  [the longest x1 5.58 us: body(): pl.pallas_call(drag_kernel, out_shape=(jax.ShapeDtypeStruct((cells_x, cel...]
    reduce_sum x2 -> x0, other arithmetic: 6.55 us -> none  [the longest x1 6.51 us: drag_group(): jnp.sum(weight_at[None] * flow_at, axis=2)]
    slice x7 -> x0, local copies, waits for them, and re-layouts: 4.38 us -> none  [the longest x1 4.34 us: body(): velocity_wide = fields_wide[:3]]
    ppermute x8 -> x4, waiting for transfers between devices: 12.9 us -> 8.75 us  [the longest x2 8.65 us: both_ways(): lax.ppermute(down, axis, [((i + 1) % count, i) for i in range(count)])]
    unnamed x13, local copies, waits for them, and re-layouts: 1.2 us -> 4.57 us
  transfers between devices with their start and end apart: 8 -> 4, of which waited for: 4 -> 3; matrix products, arithmetic and copies ran while one was open for 0% -> 1% of each run, Pallas kernels for 0% -> 0%
where the time goes in v1:
time: 49.1 us; the launch traced here: 48.6 us
  starting transfers between devices  22.8 us (46%)
  Pallas kernels  11.2 us (23%)
  waiting for transfers between devices  8.75 us (18%)
  local copies, waits for them, and re-layouts  4.57 us (9%)
  between operations  1.33 us (3%)
    ppermute x2, starting transfers between devices, both_ways(): lax.ppermute(down, axis, [((i + 1) % count, i) for i in range(count)])  12.7 us
    ppermute x2, starting transfers between devices, both_ways(): below = lax.ppermute(up, axis, [(i, (i + 1) % count) for i in range(count)])  10.1 us
    ppermute x2, waiting for transfers between devices, both_ways(): lax.ppermute(down, axis, [((i + 1) % count, i) for i in range(count)])  8.65 us
    pallas_call x1, Pallas kernels, body(): pl.pallas_call(drag_kernel, out_shape=(jax.ShapeDtypeStruct((cells_x, cel...  5.58 us
    unnamed x13, local copies, waits for them, and re-layouts  4.57 us
    pallas_call x1, Pallas kernels, body(): pl.pallas_call(deposit_kernel, out_shape=(rows_of(tile_rows), rows_of(x_r...  4.08 us
    pallas_call x1, Pallas kernels, body(): pl.pallas_call(middle_kernel, out_shape=(rows_of(tile_rows), rows_of(y_ro...  1.55 us
  transfers between devices with their start and end apart: 4, of which 3 were waited for; matrix products, arithmetic and copies ran while one was open for 1% of the time, Pallas kernels for 0%

profile of v1, /device:TPU:6, one launch (start us, length us, event | category | flops | bytes accessed | tf_op | source)
XLA Modules:
  0.0 48.6 jit_solution(2699107481522076334)
XLA Ops:
  0.6 1.4 %copy.12 = s32[1,1,4,29,128]{4,3,2,1,0:T(8,128)} copy(s32[1,1,4,29,128]{4,2,3,1,0:T(4,128)} %param.8) | data formatting | bytes 118784 | tf_op args[3]
  2.7 4.1 %deposit.1 = (f32[112,128]{1,0:T(8,128)}, f32[88,128]{1,0:T(8,128)}, f32[88,128]{1,0:T(8,128)}) custom-call(s32[1,1]{1,0:T(1,128)S(6)} %copy.14.live_ref, s32[4,29,128]{2,1,0:T(8,128)} %bitcast.8, f32[4,128]{1,0:T(4,128)} %bitcast.11, f32[3,4,16,128]{3,2,1,0:T(8,128)} %velocity_ref.5), custom_call_target="tpu_custom_call" | custom-call | tf_op jit(solution)/shard_map/deposit/pallas_call | solution.py:228
  6.8 1.9 %collective-permute-start = (f32[88,128]{1,0:T(8,128)}, f32[88,128]{1,0:T(8,128)S(1)}, u32[]{:S(2)}, u32[]{:S(2)}) collective-permute-start(f32[88,128]{1,0:T(8,128)} %get-tuple-element.11), channel_id=1, source_target_pairs={{0,8},{8,16},{16,24},{24,32},{32,40},{40,48},{48,56},{56,64},{64,7... | collective-permute-start | bytes 135176 | tf_op jit(solution)/shard_map/ppermute | solution.py:217
  8.7 10.2 %collective-permute-start.1 = (f32[88,128]{1,0:T(8,128)}, f32[88,128]{1,0:T(8,128)S(1)}, u32[]{:S(2)}, u32[]{:S(2)}) collective-permute-start(f32[88,128]{1,0:T(8,128)} %get-tuple-element.12), channel_id=1, source_target_pairs={{8,0},{16,8},{24,16},{32,24},{40,32},{48,40},{56,48},{64,56},{72,6... | collective-permute-start | bytes 135176 | tf_op jit(solution)/shard_map/ppermute | solution.py:218
  19.0 0.1 collective-permute-done.below_ref.x_below_ref
  19.1 0.0 copy-start
  19.1 1.9 %collective-permute-done.1.above_ref.x_above_ref = f32[88,128]{1,0:T(8,128)S(1)} collective-permute-done((f32[88,128]{1,0:T(8,128)}, f32[88,128]{1,0:T(8,128)S(1)}, u32[]{:S(2)}, u32[]{:S(2)}) %collective-permute-start.1) | collective-permute-done | bytes 45088 | tf_op jit(solution)/shard_map/ppermute | solution.py:218
  21.0 0.0 copy-start.1
  21.0 0.0 copy-done
  21.0 0.6 %copy-done.1 = f32[88,128]{1,0:T(8,128)} copy-done((f32[88,128]{1,0:T(8,128)}, f32[88,128]{1,0:T(8,128)S(1)}, u32[]{:S(2)}) %copy-start.1) | copy-done | bytes 45080
  21.6 0.0 copy-start.4
  21.6 1.5 %middle.1 = (f32[112,128]{1,0:T(8,128)}, f32[40,128]{1,0:T(8,128)}, f32[40,128]{1,0:T(8,128)}) custom-call(f32[112,128]{1,0:T(8,128)} %get-tuple-element.10.tile_ref, f32[3,4,16,128]{3,2,1,0:T(8,128)} %velocity_ref.5, f32[88,128]{1,0:T(8,128)} %copy-done, f32[88,128]{1,0:T(8,128)} %copy-done.1), custom_call_target="tpu_custom_call" | custom-call | tf_op jit(solution)/shard_map/middle/pallas_call | solution.py:236
  23.2 8.2 %collective-permute-start.2 = (f32[40,128]{1,0:T(8,128)}, f32[40,128]{1,0:T(8,128)S(1)}, u32[]{:S(2)}, u32[]{:S(2)}) collective-permute-start(f32[40,128]{1,0:T(8,128)} %get-tuple-element.14), channel_id=1, source_target_pairs={{0,1},{1,2},{2,3},{3,4},{4,5},{5,6},{6,7},{7,0},{8,9},{9,10},{10,1... | collective-permute-start | bytes 61448 | tf_op jit(solution)/shard_map/ppermute | solution.py:217
  31.4 2.4 %collective-permute-start.3 = (f32[40,128]{1,0:T(8,128)}, f32[40,128]{1,0:T(8,128)S(1)}, u32[]{:S(2)}, u32[]{:S(2)}) collective-permute-start(f32[40,128]{1,0:T(8,128)} %get-tuple-element.15), channel_id=1, source_target_pairs={{1,0},{2,1},{3,2},{4,3},{5,4},{6,5},{7,6},{0,7},{9,8},{10,9},{11,1... | collective-permute-start | bytes 61448 | tf_op jit(solution)/shard_map/ppermute | solution.py:218
  33.8 0.0 copy-done.4
  33.8 0.6 %copy.13 = f32[1,1,4,3,128]{4,3,2,1,0:T(4,128)} copy(f32[1,1,4,3,128]{4,2,3,1,0:T(4,128)S(1)} %copy-done.4) | data formatting | bytes 12288 | tf_op args[1]
  34.4 0.0 collective-permute-done.2.y_below_ref
  34.4 0.0 copy-start.2
  34.4 6.7 %collective-permute-done.3.y_above_ref = f32[40,128]{1,0:T(8,128)S(1)} collective-permute-done((f32[40,128]{1,0:T(8,128)}, f32[40,128]{1,0:T(8,128)S(1)}, u32[]{:S(2)}, u32[]{:S(2)}) %collective-permute-start.3) | collective-permute-done | bytes 20512 | tf_op jit(solution)/shard_map/ppermute | solution.py:218
  41.2 0.0 copy-start.3
  41.2 0.0 copy-done.2
  41.2 0.6 %copy-done.3 = f32[40,128]{1,0:T(8,128)} copy-done((f32[40,128]{1,0:T(8,128)}, f32[40,128]{1,0:T(8,128)S(1)}, u32[]{:S(2)}) %copy-start.3) | copy-done | bytes 20504
  41.8 5.6 %drag.1 = (f32[4,16,128]{2,1,0:T(8,128)}, f32[4,3,128]{2,1,0:T(4,128)}) custom-call(s32[1,1]{1,0:T(1,128)S(6)} %copy.14.live_ref, s32[4,29,128]{2,1,0:T(8,128)} %bitcast.9, f32[4,128]{1,0:T(4,128)} %bitcast.12, f32[4,3,128]{2,1,0:T(4,128)} %bitcast.10, f32[3,4,16,128]{3,2,1,0:T(8,128)} %velocity_ref.5, f32[112,128]{1,0:T(8,128)} %get-tuple-element.13.tile_ref, ...), custom_call_target="tpu_custom_call" | custom-call | tf_op jit(solution)/shard_map/drag/pallas_call | solution.py:244
  47.4 1.3 %copy.9 = f32[1,1,4,3,128]{4,2,3,1,0:T(4,128)} copy(f32[1,1,4,3,128]{4,3,2,1,0:T(4,128)} %bitcast.13) | data formatting | bytes 12288
Async XLA Ops:
  6.8 12.3 %collective-permute-start = (f32[88,128]{1,0:T(8,128)}, f32[88,128]{1,0:T(8,128)S(1)}, u32[]{:S(2)}, u32[]{:S(2)}) collective-permute-start(f32[88,128]{1,0:T(8,128)} %get-tuple-element.11), channel_id=1, source_target_pairs={{0,8},{8,16},{16,24},{24,32},{32,40},{40,48},{48,56},{56,64},{64,7... | collective-permute-start | bytes 135176 | tf_op jit(solution)/shard_map/ppermute | solution.py:217
  8.7 12.3 %collective-permute-start.1 = (f32[88,128]{1,0:T(8,128)}, f32[88,128]{1,0:T(8,128)S(1)}, u32[]{:S(2)}, u32[]{:S(2)}) collective-permute-start(f32[88,128]{1,0:T(8,128)} %get-tuple-element.12), channel_id=1, source_target_pairs={{8,0},{16,8},{24,16},{32,24},{40,32},{48,40},{56,48},{64,56},{72,6... | collective-permute-start | bytes 135176 | tf_op jit(solution)/shard_map/ppermute | solution.py:218
  19.1 1.9 %copy-start = (f32[88,128]{1,0:T(8,128)}, f32[88,128]{1,0:T(8,128)S(1)}, u32[]{:S(2)}) copy-start(f32[88,128]{1,0:T(8,128)S(1)} %collective-permute-done.below_ref.x_below_ref) | copy-start | bytes 135172
  21.0 0.6 %copy-start.1 = (f32[88,128]{1,0:T(8,128)}, f32[88,128]{1,0:T(8,128)S(1)}, u32[]{:S(2)}) copy-start(f32[88,128]{1,0:T(8,128)S(1)} %collective-permute-done.1.above_ref.x_above_ref) | copy-start | bytes 135172
  21.6 12.2 %copy-start.4 = (f32[1,1,4,3,128]{4,2,3,1,0:T(4,128)S(1)}, f32[1,1,4,3,128]{4,2,3,1,0:T(4,128)}, u32[]{:S(2)}) copy-start(f32[1,1,4,3,128]{4,2,3,1,0:T(4,128)} %param.6) | copy-start | bytes 18436
  23.2 11.3 %collective-permute-start.2 = (f32[40,128]{1,0:T(8,128)}, f32[40,128]{1,0:T(8,128)S(1)}, u32[]{:S(2)}, u32[]{:S(2)}) collective-permute-start(f32[40,128]{1,0:T(8,128)} %get-tuple-element.14), channel_id=1, source_target_pairs={{0,1},{1,2},{2,3},{3,4},{4,5},{5,6},{6,7},{7,0},{8,9},{9,10},{10,1... | collective-permute-start | bytes 61448 | tf_op jit(solution)/shard_map/ppermute | solution.py:217
  31.4 9.8 %collective-permute-start.3 = (f32[40,128]{1,0:T(8,128)}, f32[40,128]{1,0:T(8,128)S(1)}, u32[]{:S(2)}, u32[]{:S(2)}) collective-permute-start(f32[40,128]{1,0:T(8,128)} %get-tuple-element.15), channel_id=1, source_target_pairs={{1,0},{2,1},{3,2},{4,3},{5,4},{6,5},{7,6},{0,7},{9,8},{10,9},{11,1... | collective-permute-start | bytes 61448 | tf_op jit(solution)/shard_map/ppermute | solution.py:218
  34.4 6.8 %copy-start.2 = (f32[40,128]{1,0:T(8,128)}, f32[40,128]{1,0:T(8,128)S(1)}, u32[]{:S(2)}) copy-start(f32[40,128]{1,0:T(8,128)S(1)} %collective-permute-done.2.y_below_ref) | copy-start | bytes 61444
  41.2 0.6 %copy-start.3 = (f32[40,128]{1,0:T(8,128)}, f32[40,128]{1,0:T(8,128)S(1)}, u32[]{:S(2)}) copy-start(f32[40,128]{1,0:T(8,128)S(1)} %collective-permute-done.3.y_above_ref) | copy-start | bytes 61444

commit v2 on v0

v2 whole, which is shorter than its diff:
```python
import jax
import jax.numpy as jnp
from jax import lax
from jax.experimental import pallas as pl
from jax.experimental.pallas import tpu as pltpu
from jax.sharding import PartitionSpec as P

exponent = -2.65
drag_scale = 2.0
void_floor = 0.1

cells_x, cells_y, cells_z = 4, 16, 128
wide_x, wide_y = cells_x + 2, cells_y + 2
own_y = wide_y - 4
late_rows = 4 * wide_x
early_rows = wide_x * own_y
early_padded = 88
tile_rows = 112
x_rows, x_flow, y_rows, y_flow = 88, 40, 40, 16


def split_cells(cells):
    lane = cells & (cells_z - 1)
    column = cells >> 7
    i = (column * 3641) >> 16
    j = column - i * wide_y
    late = jnp.where(j < 2, j, j - own_y) * wide_x + i
    early = late_rows + i * own_y + (j - 2)
    row = jnp.where((j < 2) | (j >= wide_y - 2), late, early)
    return row, lane


def points_in(cells_ref, block):
    return jnp.concatenate([cells_ref[s, block : block + 1] for s in range(cells_ref.shape[0])], axis=0)


def halves(value):
    high = value.astype(jnp.bfloat16)
    low = (value - high.astype(jnp.float32)).astype(jnp.bfloat16)
    return high, low


def counted(rows):
    return lax.broadcasted_iota(jnp.int32, (rows, 128), 0)


def narrow(value):
    return value.astype(jnp.float32).astype(jnp.bfloat16)


def pairs_of(block, points):
    every = [(block, s) for s in range(points)]
    return [every[at : at + 2] for at in range(0, points, 2)]


def deposit_kernel(
    live_ref, cells_ref, volume_ref, velocity_ref, tile_ref, up_ref, down_ref, share_ref, cells_in, volume_in, live_in, sems
):
    points, blocks = cells_ref.shape[0], cells_ref.shape[1]
    copies = [
        pltpu.make_async_copy(cells_ref, cells_in, sems.at[0]),
        pltpu.make_async_copy(volume_ref, volume_in, sems.at[1]),
        pltpu.make_async_copy(live_ref, live_in, sems.at[2]),
    ]
    for f in range(3):
        at = pl.ds(x_flow + cells_y * f, cells_y)
        copies.append(pltpu.make_async_copy(velocity_ref.at[f, cells_x - 1], up_ref.at[at], sems.at[3 + f]))
        copies.append(pltpu.make_async_copy(velocity_ref.at[f, 0], down_ref.at[at], sems.at[6 + f]))
    for copy in copies:
        copy.start()
    row_at = narrow(counted(tile_rows))
    lane_at = narrow(counted(cells_z))
    one = jnp.ones((), jnp.bfloat16)
    zero = jnp.zeros((), jnp.bfloat16)
    copies[1].wait()
    share = volume_in[...] / points
    high, low = halves(share)
    copies[0].wait()
    totals = []
    for b in range(blocks):
        row, lane = split_cells(points_in(cells_in, b))
        row, lane = narrow(row), narrow(lane)
        total = jnp.zeros((2 * tile_rows, cells_z), jnp.float32)
        for pair in pairs_of(b, points):
            left, right = [], []
            for _, s in pair:
                at_row = row_at == row[s : s + 1]
                left.append(
                    jnp.concatenate(
                        [jnp.where(at_row, high[b : b + 1], zero), jnp.where(at_row, low[b : b + 1], zero)], axis=0
                    )
                )
                right.append(jnp.where(lane_at == lane[s : s + 1], one, zero))
            total += lax.dot_general(
                jnp.concatenate(left, axis=1),
                jnp.concatenate(right, axis=1),
                (((1,), (1,)), ((), ())),
                preferred_element_type=jnp.float32,
            )
        totals.append(total)
    copies[2].wait()
    live = live_in[0, 0]
    tile = jnp.zeros((tile_rows, cells_z), jnp.float32)
    for b in range(blocks):
        alive = jnp.where(b < live, 1.0, 0.0)
        tile += alive * (totals[b][:tile_rows] + totals[b][tile_rows:])
        share_ref[b : b + 1] = alive * share[b : b + 1]
    tile_ref[...] = tile
    up_ref[0:28] = tile_ref[80:108]
    down_ref[0:28] = tile_ref[24:52]
    for g in range(4):
        up_ref[28 + 2 * g : 30 + 2 * g] = tile_ref[6 * g + 4 : 6 * g + 6]
        down_ref[28 + 2 * g : 30 + 2 * g] = tile_ref[6 * g : 6 * g + 2]
    up_ref[36:40] = jnp.zeros((4, 128), jnp.float32)
    down_ref[36:40] = jnp.zeros((4, 128), jnp.float32)
    for copy in copies[3:]:
        copy.wait()


def middle_kernel(tile_ref, velocity_ref, below_ref, above_ref, out_ref, up_ref, down_ref):
    out_ref[...] = tile_ref[...]
    out_ref[24:52] += below_ref[0:28]
    out_ref[80:108] += above_ref[0:28]
    for g in range(4):
        out_ref[6 * g : 6 * g + 2] += below_ref[28 + 2 * g : 30 + 2 * g]
        out_ref[6 * g + 4 : 6 * g + 6] += above_ref[28 + 2 * g : 30 + 2 * g]

    def fill(dest_ref, first, near):
        dest_ref[...] = jnp.zeros((y_rows, 128), jnp.float32)
        dest_ref[0:12] = out_ref[first : first + 12]
        for f in range(3):
            at, halo = y_flow + 8 * f, x_flow + cells_y * f + near
            dest_ref[at : at + 1] = below_ref[halo : halo + 1]
            for i in range(cells_x):
                dest_ref[at + 1 + i : at + 2 + i] = velocity_ref[f, i, near : near + 1]
            dest_ref[at + 5 : at + 6] = above_ref[halo : halo + 1]

    fill(up_ref, 12, cells_y - 1)
    fill(down_ref, 0, 0)


def looked_up(cells_ref, fields, first):
    points, blocks = cells_ref.shape[0], cells_ref.shape[1]
    rows = fields[0].shape[0]
    table = jnp.concatenate(list(halves(jnp.concatenate(fields, axis=0))), axis=1)
    row_at = counted(rows) + first
    lane_at = narrow(counted(cells_z))
    one = jnp.ones((), jnp.bfloat16)
    zero = jnp.zeros((), jnp.bfloat16)
    sums = []
    for b in range(blocks):
        row, lane = split_cells(points_in(cells_ref, b))
        lane = narrow(lane)
        part_sums = [jnp.zeros((8, 128), jnp.float32) for _ in fields]
        for pair in pairs_of(b, points):
            right = [jnp.where(lane_at == lane[s : s + 1], one, zero) for _, s in pair]
            right = jnp.concatenate(right, axis=1)
            found = jnp.dot(table, jnp.concatenate([right, right], axis=0), preferred_element_type=jnp.float32)
            for n, (_, s) in enumerate(pair):
                at_row = row_at == row[s : s + 1]
                for f in range(len(fields)):
                    part = jnp.where(at_row, found[f * rows : (f + 1) * rows, n * 128 : n * 128 + 128], 0.0)
                    part_sums[f] = part_sums[f] + jnp.sum(part.reshape(rows // 8, 8, 128), axis=0)
        sums.append([jnp.sum(part, axis=0, keepdims=True) for part in part_sums])
    return sums


def void_of(solid):
    return jnp.maximum(1.0 - solid, void_floor)


def resistance_of(void):
    return jnp.exp(exponent * jnp.log(void))


def early_kernel(cells_ref, velocity_ref, tile_ref, below_ref, above_ref, sums_ref):
    resistance = resistance_of(void_of(tile_ref[late_rows : late_rows + early_rows]))
    fields = [resistance]
    for f in range(3):
        halo = x_flow + cells_y * f + 1
        flow = [below_ref[halo : halo + own_y]]
        flow += [velocity_ref[f, i, 1 : 1 + own_y] for i in range(cells_x)]
        flow += [above_ref[halo : halo + own_y]]
        fields.append(resistance * jnp.concatenate(flow, axis=0))
    blank = jnp.zeros((early_padded - early_rows, 128), jnp.float32)
    fields = [jnp.concatenate([field, blank], axis=0) for field in fields]
    for b, sums in enumerate(looked_up(cells_ref, fields, late_rows)):
        for f in range(4):
            sums_ref[f, b : b + 1] = sums[f]


def drag_kernel(
    cells_ref, share_ref, particle_ref, tile_ref, up_ref, down_ref, below_ref, above_ref, sums_ref, void_ref, drag_ref
):
    late = jnp.concatenate(
        [tile_ref[0:12] + below_ref[0:12], tile_ref[12:24] + above_ref[0:12]], axis=0
    )
    late_void = void_of(late)
    early_void = void_of(tile_ref[late_rows : late_rows + early_rows])
    for i in range(1, cells_x + 1):
        void_ref[i - 1, 0:1] = late_void[wide_x + i : wide_x + i + 1]
        void_ref[i - 1, 1 : 1 + own_y] = early_void[i * own_y : (i + 1) * own_y]
        void_ref[i - 1, 1 + own_y : 2 + own_y] = late_void[2 * wide_x + i : 2 * wide_x + i + 1]
    resistance = resistance_of(late_void)
    fields = [resistance]
    for f in range(3):
        at = slice(y_flow + 8 * f, y_flow + 8 * f + wide_x)
        flow = jnp.concatenate([below_ref[at], down_ref[at], up_ref[at], above_ref[at]], axis=0)
        fields.append(resistance * flow)
    for b, sums in enumerate(looked_up(cells_ref, fields, 0)):
        total = [sums[f] + sums_ref[f, b : b + 1] for f in range(4)]
        for f in range(3):
            force = total[f + 1] - particle_ref[f, b : b + 1] * total[0]
            drag_ref[f, b : b + 1] = drag_scale * share_ref[b : b + 1] * force


def on_chip(count):
    return [pl.BlockSpec(memory_space=pltpu.VMEM)] * count


def array_of(*shape):
    return jax.ShapeDtypeStruct(shape, jnp.float32)


def both_ways(up, down, axis):
    count = lax.axis_size(axis)
    below = lax.ppermute(up, axis, [(i, (i + 1) % count) for i in range(count)])
    above = lax.ppermute(down, axis, [((i + 1) % count, i) for i in range(count)])
    return below, above


def small():
    return pltpu.CompilerParams(vmem_limit_bytes=16 * 1024 * 1024)


def body(fluid_velocity, particle_velocity, particle_volume, satellite_cells, live_blocks):
    cells = jnp.transpose(satellite_cells[0, 0], (1, 0, 2))
    volume = particle_volume[0, 0]
    particles = jnp.transpose(particle_velocity[0, 0], (1, 0, 2))
    blocks = volume.shape[0]
    tile, x_up, x_down, share = pl.pallas_call(
        deposit_kernel,
        out_shape=(array_of(tile_rows, 128), array_of(x_rows, 128), array_of(x_rows, 128), array_of(blocks, 128)),
        in_specs=[pl.BlockSpec(memory_space=pltpu.HBM)] * 4,
        out_specs=tuple(on_chip(4)),
        scratch_shapes=[
            pltpu.VMEM(cells.shape, jnp.int32),
            pltpu.VMEM(volume.shape, jnp.float32),
            pltpu.SMEM(live_blocks.shape, jnp.int32),
            pltpu.SemaphoreType.DMA((9,)),
        ],
        compiler_params=small(),
        name="deposit",
    )(live_blocks, *(pltpu.with_memory_space_constraint(value, pltpu.HBM) for value in (cells, volume, fluid_velocity)))
    x_below, x_above = both_ways(x_up, x_down, "gx")
    tile, y_up, y_down = pl.pallas_call(
        middle_kernel,
        out_shape=(array_of(tile_rows, 128), array_of(y_rows, 128), array_of(y_rows, 128)),
        in_specs=on_chip(4),
        out_specs=tuple(on_chip(3)),
        compiler_params=small(),
        name="middle",
    )(tile, fluid_velocity, x_below, x_above)
    y_below, y_above = both_ways(y_up, y_down, "gy")
    sums = pl.pallas_call(
        early_kernel,
        out_shape=array_of(4, blocks, 128),
        in_specs=on_chip(5),
        out_specs=on_chip(1)[0],
        compiler_params=small(),
        cost_estimate=pl.CostEstimate(flops=3_000_000_000, bytes_accessed=300_000, transcendentals=20_000),
        name="early",
    )(cells, fluid_velocity, tile, x_below, x_above)
    void, drag = pl.pallas_call(
        drag_kernel,
        out_shape=(array_of(cells_x, cells_y, cells_z), array_of(3, blocks, 128)),
        in_specs=on_chip(9),
        out_specs=tuple(on_chip(2)),
        compiler_params=small(),
        name="drag",
    )(cells, share, particles, tile, y_up, y_down, y_below, y_above, sums)
    return void, jnp.transpose(drag, (1, 0, 2))[None, None]


def solution(mesh):
    placed = (
        P(None, "gx", "gy", None),
        P("gx", "gy", None, None, None),
        P("gx", "gy", None, None),
        P("gx", "gy", None, None, None),
        P("gx", "gy"),
    )
    return jax.shard_map(
        body,
        mesh=mesh,
        in_specs=placed,
        out_specs=(P("gx", "gy", None), P("gx", "gy", None, None, None)),
        check_vma=False,
    )
```

time: 264 us -> 38.2 us (0.14)
  local copies, waits for them, and re-layouts: 115 us -> 0.01 us
  other arithmetic: 90.6 us -> 0 us
  starting transfers between devices: 42.8 us -> 22.8 us
  Pallas kernels: 0 us -> 7.94 us
  waiting for transfers between devices: 12.9 us -> 5.73 us
    gather x3 -> x0, local copies, waits for them, and re-layouts: 107 us -> none  [the longest x2 76.4 us: drag_group(): weight_at = jnp.take(resistance, satellites)]
    scatter-add x5 -> x0, other arithmetic: 81 us -> none  [the longest x1 80.9 us: deposit(): return deposit_tile.at[satellites.reshape(-1)].add(weights.reshape(-1))]
    ppermute x8 -> x4, starting transfers between devices: 42.8 us -> 22.8 us  [the longest x2 12.7 us: both_ways(): lax.ppermute(down, axis, [((i + 1) % count, i) for i in range(count)])]
    pallas_call x0 -> x4, Pallas kernels: none -> 7.94 us  [the longest x1 3.07 us: body(): pl.pallas_call(early_kernel, out_shape=array_of(4, blocks, 128), in_specs...]
    ppermute x8 -> x4, waiting for transfers between devices: 12.9 us -> 5.73 us  [the longest x2 5.73 us: both_ways(): lax.ppermute(down, axis, [((i + 1) % count, i) for i in range(count)])]
    reduce_sum x2 -> x0, other arithmetic: 6.55 us -> none  [the longest x1 6.51 us: drag_group(): jnp.sum(weight_at[None] * flow_at, axis=2)]
    slice x7 -> x0, local copies, waits for them, and re-layouts: 4.38 us -> none  [the longest x1 4.34 us: body(): velocity_wide = fields_wide[:3]]
  transfers between devices with their start and end apart: 8 -> 4, of which waited for: 4 -> 2; matrix products, arithmetic and copies ran while one was open for 0% -> 0% of each run, Pallas kernels for 0% -> 8%
where the time goes in v2:
time: 38.2 us; the launch traced here: 37.9 us
  starting transfers between devices  22.8 us (60%)
  Pallas kernels  7.94 us (21%)
  waiting for transfers between devices  5.73 us (15%)
  between operations  1.4 us (4%)
    ppermute x2, starting transfers between devices, both_ways(): lax.ppermute(down, axis, [((i + 1) % count, i) for i in range(count)])  12.7 us
    ppermute x2, starting transfers between devices, both_ways(): below = lax.ppermute(up, axis, [(i, (i + 1) % count) for i in range(count)])  10.1 us
    ppermute x2, waiting for transfers between devices, both_ways(): lax.ppermute(down, axis, [((i + 1) % count, i) for i in range(count)])  5.73 us
    pallas_call x1, Pallas kernels, body(): pl.pallas_call(early_kernel, out_shape=array_of(4, blocks, 128), in_specs...  3.07 us
    pallas_call x1, Pallas kernels, body(): pl.pallas_call(deposit_kernel, out_shape=(array_of(tile_rows, 128), array...  2.87 us
    pallas_call x1, Pallas kernels, body(): pl.pallas_call(drag_kernel, out_shape=(array_of(cells_x, cells_y, cells_z...  1.97 us
  transfers between devices with their start and end apart: 4, of which 2 were waited for; matrix products, arithmetic and copies ran while one was open for 0% of the time, Pallas kernels for 8%

profile of v2, /device:TPU:6, one launch (start us, length us, event | category | flops | bytes accessed | tf_op | source)
XLA Modules:
  0.0 37.9 jit_solution(9571552590758535945)
XLA Ops:
  0.6 0.0 copy-start
  1.3 2.9 %deposit.1 = (f32[112,128]{1,0:T(8,128)S(1)}, f32[88,128]{1,0:T(8,128)S(1)}, f32[88,128]{1,0:T(8,128)S(1)}, f32[4,128]{1,0:T(4,128)S(1)}) custom-call(s32[1,1]{1,0:T(1,128)S(6)} %copy.7.live_ref, s32[29,4,128]{2,1,0:T(4,128)} %bitcast.10, f32[4,128]{1,0:T(4,128)} %bitcast.14, f32[3,4,16,128]{3,2,1,0:T(8,128)} %velocity_ref.5), custom_call_target="tpu_custom_call" | custom-call | tf_op jit(solution)/shard_map/deposit/pallas_call | solution.py:241
  4.2 1.9 %collective-permute-start = (f32[88,128]{1,0:T(8,128)S(1)}, f32[88,128]{1,0:T(8,128)S(1)}, u32[]{:S(2)}, u32[]{:S(2)}) collective-permute-start(f32[88,128]{1,0:T(8,128)S(1)} %get-tuple-element.13), channel_id=1, source_target_pairs={{0,8},{8,16},{16,24},{24,32},{32,40},{40,48},{48,56},{56,64},{64,7... | collective-permute-start | bytes 135176 | tf_op jit(solution)/shard_map/ppermute | solution.py:227
  6.1 10.2 %collective-permute-start.1 = (f32[88,128]{1,0:T(8,128)S(1)}, f32[88,128]{1,0:T(8,128)S(1)}, u32[]{:S(2)}, u32[]{:S(2)}) collective-permute-start(f32[88,128]{1,0:T(8,128)S(1)} %get-tuple-element.14), channel_id=1, source_target_pairs={{8,0},{16,8},{24,16},{32,24},{40,32},{48,40},{56,48},{64,56},{72,6... | collective-permute-start | bytes 135176 | tf_op jit(solution)/shard_map/ppermute | solution.py:228
  16.4 0.0 collective-permute-done.below_ref
  16.4 1.7 %collective-permute-done.1.above_ref = f32[88,128]{1,0:T(8,128)S(1)} collective-permute-done((f32[88,128]{1,0:T(8,128)S(1)}, f32[88,128]{1,0:T(8,128)S(1)}, u32[]{:S(2)}, u32[]{:S(2)}) %collective-permute-start.1) | collective-permute-done | bytes 45088 | tf_op jit(solution)/shard_map/ppermute | solution.py:228
  18.1 0.0 copy-done
  18.1 0.0 copy-start.1
  18.1 8.2 %collective-permute-start.2 = (f32[40,128]{1,0:T(8,128)S(1)}, f32[40,128]{1,0:T(8,128)S(1)}, u32[]{:S(2)}, u32[]{:S(2)}) collective-permute-start(f32[40,128]{1,0:T(8,128)S(1)} %get-tuple-element.16.up_ref), channel_id=1, source_target_pairs={{0,1},{1,2},{2,3},{3,4},{4,5},{5,6},{6,7},{7,0},{8,9},{9,10},{10,1... | collective-permute-start | bytes 61448 | tf_op jit(solution)/shard_map/ppermute | solution.py:227
  26.3 2.4 %collective-permute-start.3 = (f32[40,128]{1,0:T(8,128)S(1)}, f32[40,128]{1,0:T(8,128)S(1)}, u32[]{:S(2)}, u32[]{:S(2)}) collective-permute-start(f32[40,128]{1,0:T(8,128)S(1)} %get-tuple-element.17.down_ref), channel_id=1, source_target_pairs={{1,0},{2,1},{3,2},{4,3},{5,4},{6,5},{7,6},{0,7},{9,8},{10,9},{11,1... | collective-permute-start | bytes 61448 | tf_op jit(solution)/shard_map/ppermute | solution.py:228
  28.8 0.0 copy-done.1
  28.8 0.0 copy-start.2
  28.8 3.1 %early.1.sums_ref = f32[4,4,128]{2,1,0:T(4,128)S(1)} custom-call(s32[29,4,128]{2,1,0:T(4,128)S(1)} %bitcast.11, f32[3,4,16,128]{3,2,1,0:T(8,128)S(1)} %copy-done, f32[112,128]{1,0:T(8,128)S(1)} %get-tuple-element.15.tile_ref, f32[88,128]{1,0:T(8,128)S(1)} %collective-permute-done.below_ref, f32[88,128]{1,0:T(8,128)S(1)} %collective-permute-done.1.above_ref), custom_call_target="tpu_custom_call" | custom-call | flops 3000000000 | bytes 300000 | tf_op jit(solution)/shard_map/early/pallas_call | solution.py:265
  31.9 0.0 collective-permute-done.2.below_ref
  31.9 4.0 %collective-permute-done.3.above_ref = f32[40,128]{1,0:T(8,128)S(1)} collective-permute-done((f32[40,128]{1,0:T(8,128)S(1)}, f32[40,128]{1,0:T(8,128)S(1)}, u32[]{:S(2)}, u32[]{:S(2)}) %collective-permute-start.3) | collective-permute-done | bytes 20512 | tf_op jit(solution)/shard_map/ppermute | solution.py:228
  35.9 0.0 copy-done.2
  35.9 2.0 %drag.1 = (f32[4,16,128]{2,1,0:T(8,128)}, f32[3,4,128]{2,1,0:T(4,128)}) custom-call(s32[29,4,128]{2,1,0:T(4,128)S(1)} %bitcast.12, f32[4,128]{1,0:T(4,128)S(1)} %get-tuple-element.11.share_ref, f32[3,4,128]{2,1,0:T(4,128)S(1)} %bitcast.13, f32[112,128]{1,0:T(8,128)S(1)} %get-tuple-element.15.tile_ref, f32[40,128]{1,0:T(8,128)S(1)} %get-tuple-element.16.up_ref, ...), custom_call_target="tpu_custom_call" | custom-call | tf_op jit(solution)/shard_map/drag/pallas_call | solution.py:274
  (1 shorter events, 0.0 us)
Async XLA Ops:
  0.6 17.4 %copy-start = (f32[3,4,16,128]{3,2,1,0:T(8,128)S(1)}, f32[3,4,16,128]{3,2,1,0:T(8,128)}, u32[]{:S(2)}) copy-start(f32[3,4,16,128]{3,2,1,0:T(8,128)} %velocity_ref.5) | copy-start | bytes 294916
  4.2 12.2 %collective-permute-start = (f32[88,128]{1,0:T(8,128)S(1)}, f32[88,128]{1,0:T(8,128)S(1)}, u32[]{:S(2)}, u32[]{:S(2)}) collective-permute-start(f32[88,128]{1,0:T(8,128)S(1)} %get-tuple-element.13), channel_id=1, source_target_pairs={{0,8},{8,16},{16,24},{24,32},{32,40},{40,48},{48,56},{56,64},{64,7... | collective-permute-start | bytes 135176 | tf_op jit(solution)/shard_map/ppermute | solution.py:227
  6.1 11.9 %collective-permute-start.1 = (f32[88,128]{1,0:T(8,128)S(1)}, f32[88,128]{1,0:T(8,128)S(1)}, u32[]{:S(2)}, u32[]{:S(2)}) collective-permute-start(f32[88,128]{1,0:T(8,128)S(1)} %get-tuple-element.14), channel_id=1, source_target_pairs={{8,0},{16,8},{24,16},{32,24},{40,32},{48,40},{56,48},{64,56},{72,6... | collective-permute-start | bytes 135176 | tf_op jit(solution)/shard_map/ppermute | solution.py:228
  18.1 10.7 %copy-start.1 = (s32[1,1,4,29,128]{4,2,3,1,0:T(4,128)S(1)}, s32[1,1,4,29,128]{4,2,3,1,0:T(4,128)}, u32[]{:S(2)}) copy-start(s32[1,1,4,29,128]{4,2,3,1,0:T(4,128)} %param.8) | copy-start | bytes 178180
  18.1 13.8 %collective-permute-start.2 = (f32[40,128]{1,0:T(8,128)S(1)}, f32[40,128]{1,0:T(8,128)S(1)}, u32[]{:S(2)}, u32[]{:S(2)}) collective-permute-start(f32[40,128]{1,0:T(8,128)S(1)} %get-tuple-element.16.up_ref), channel_id=1, source_target_pairs={{0,1},{1,2},{2,3},{3,4},{4,5},{5,6},{6,7},{7,0},{8,9},{9,10},{10,1... | collective-permute-start | bytes 61448 | tf_op jit(solution)/shard_map/ppermute | solution.py:227
  26.3 9.6 %collective-permute-start.3 = (f32[40,128]{1,0:T(8,128)S(1)}, f32[40,128]{1,0:T(8,128)S(1)}, u32[]{:S(2)}, u32[]{:S(2)}) collective-permute-start(f32[40,128]{1,0:T(8,128)S(1)} %get-tuple-element.17.down_ref), channel_id=1, source_target_pairs={{1,0},{2,1},{3,2},{4,3},{5,4},{6,5},{7,6},{0,7},{9,8},{10,9},{11,1... | collective-permute-start | bytes 61448 | tf_op jit(solution)/shard_map/ppermute | solution.py:228
  28.8 7.1 %copy-start.2 = (f32[1,1,4,3,128]{4,2,3,1,0:T(4,128)S(1)}, f32[1,1,4,3,128]{4,2,3,1,0:T(4,128)}, u32[]{:S(2)}) copy-start(f32[1,1,4,3,128]{4,2,3,1,0:T(4,128)} %param.6) | copy-start | bytes 18436

commit v3 on v2

--- a/solution.py
+++ b/solution.py
@@ -1,9 +1,12 @@
+import functools
+
 import jax
 import jax.numpy as jnp
 from jax import lax
 from jax.experimental import pallas as pl
 from jax.experimental.pallas import tpu as pltpu
 from jax.sharding import PartitionSpec as P
+
 
 exponent = -2.65
 drag_scale = 2.0
@@ -173,45 +176,64 @@
     return jnp.exp(exponent * jnp.log(void))
 
 
-def early_kernel(cells_ref, velocity_ref, tile_ref, below_ref, above_ref, sums_ref):
-    resistance = resistance_of(void_of(tile_ref[late_rows : late_rows + early_rows]))
-    fields = [resistance]
-    for f in range(3):
-        halo = x_flow + cells_y * f + 1
-        flow = [below_ref[halo : halo + own_y]]
-        flow += [velocity_ref[f, i, 1 : 1 + own_y] for i in range(cells_x)]
-        flow += [above_ref[halo : halo + own_y]]
-        fields.append(resistance * jnp.concatenate(flow, axis=0))
-    blank = jnp.zeros((early_padded - early_rows, 128), jnp.float32)
-    fields = [jnp.concatenate([field, blank], axis=0) for field in fields]
-    for b, sums in enumerate(looked_up(cells_ref, fields, late_rows)):
-        for f in range(4):
-            sums_ref[f, b : b + 1] = sums[f]
-
-
-def drag_kernel(
-    cells_ref, share_ref, particle_ref, tile_ref, up_ref, down_ref, below_ref, above_ref, sums_ref, void_ref, drag_ref
-):
-    late = jnp.concatenate(
-        [tile_ref[0:12] + below_ref[0:12], tile_ref[12:24] + above_ref[0:12]], axis=0
-    )
-    late_void = void_of(late)
-    early_void = void_of(tile_ref[late_rows : late_rows + early_rows])
-    for i in range(1, cells_x + 1):
-        void_ref[i - 1, 0:1] = late_void[wide_x + i : wide_x + i + 1]
-        void_ref[i - 1, 1 : 1 + own_y] = early_void[i * own_y : (i + 1) * own_y]
-        void_ref[i - 1, 1 + own_y : 2 + own_y] = late_void[2 * wide_x + i : 2 * wide_x + i + 1]
-    resistance = resistance_of(late_void)
-    fields = [resistance]
-    for f in range(3):
-        at = slice(y_flow + 8 * f, y_flow + 8 * f + wide_x)
-        flow = jnp.concatenate([below_ref[at], down_ref[at], up_ref[at], above_ref[at]], axis=0)
-        fields.append(resistance * flow)
-    for b, sums in enumerate(looked_up(cells_ref, fields, 0)):
-        total = [sums[f] + sums_ref[f, b : b + 1] for f in range(4)]
+def on_side(side):
+    return lax.rem(lax.axis_index("gy"), 2) == side
+
+
+def early_kernel(side, cells_ref, velocity_ref, tile_ref, below_ref, above_ref, sums_ref):
+    @pl.when(on_side(side))
+    def _():
+        resistance = resistance_of(void_of(tile_ref[late_rows : late_rows + early_rows]))
+        fields = [resistance]
         for f in range(3):
-            force = total[f + 1] - particle_ref[f, b : b + 1] * total[0]
-            drag_ref[f, b : b + 1] = drag_scale * share_ref[b : b + 1] * force
+            halo = x_flow + cells_y * f + 1
+            flow = [below_ref[halo : halo + own_y]]
+            flow += [velocity_ref[f, i, 1 : 1 + own_y] for i in range(cells_x)]
+            flow += [above_ref[halo : halo + own_y]]
+            fields.append(resistance * jnp.concatenate(flow, axis=0))
+        blank = jnp.zeros((early_padded - early_rows, 128), jnp.float32)
+        fields = [jnp.concatenate([field, blank], axis=0) for field in fields]
+        for b, sums in enumerate(looked_up(cells_ref, fields, late_rows)):
+            for f in range(4):
+                sums_ref[f, b : b + 1] = sums[f]
+
+
+def drag_kernel(side, *refs):
+    cells_ref, share_ref, particle_ref, tile_ref, up_ref, down_ref, below_ref, above_ref, sums_ref = refs[:9]
+    void_out, drag_out, void_ref, drag_ref, particle_in, sems = refs[-6:]
+
+    @pl.when(on_side(side))
+    def _():
+        fetch = pltpu.make_async_copy(particle_ref, particle_in, sems.at[2])
+        fetch.start()
+        late = jnp.concatenate([tile_ref[0:12] + below_ref[0:12], tile_ref[12:24] + above_ref[0:12]], axis=0)
+        late_void = void_of(late)
+        early_void = void_of(tile_ref[late_rows : late_rows + early_rows])
+        for i in range(1, cells_x + 1):
+            void_ref[i - 1, 0:1] = late_void[wide_x + i : wide_x + i + 1]
+            void_ref[i - 1, 1 : 1 + own_y] = early_void[i * own_y : (i + 1) * own_y]
+            void_ref[i - 1, 1 + own_y : 2 + own_y] = late_void[2 * wide_x + i : 2 * wide_x + i + 1]
+        resistance = resistance_of(late_void)
+        fields = [resistance]
+        for f in range(3):
+            at = slice(y_flow + 8 * f, y_flow + 8 * f + wide_x)
+            flow = jnp.concatenate([below_ref[at], down_ref[at], up_ref[at], above_ref[at]], axis=0)
+            fields.append(resistance * flow)
+        found = looked_up(cells_ref, fields, 0)
+        fetch.wait()
+        for b, sums in enumerate(found):
+            total = [sums[f] + sums_ref[f, b : b + 1] for f in range(4)]
+            for f in range(3):
+                force = total[f + 1] - particle_in[f, b : b + 1] * total[0]
+                drag_ref[f, b : b + 1] = drag_scale * share_ref[b : b + 1] * force
+        copies = [
+            pltpu.make_async_copy(void_ref, void_out, sems.at[0]),
+            pltpu.make_async_copy(drag_ref, drag_out, sems.at[1]),
+        ]
+        for copy in copies:
+            copy.start()
+        for copy in copies:
+            copy.wait()
 
 
 def on_chip(count):
@@ -229,6 +251,41 @@
     return below, above
 
 
+def one_way(value, axis, side, step):
+    count = lax.axis_size(axis)
+    return lax.ppermute(value, axis, [(i, (i + step) % count) for i in range(count) if i % 2 == side])
+
+
+def early(side, values):
+    return pl.pallas_call(
+        functools.partial(early_kernel, side),
+        out_shape=array_of(4, values[0].shape[1], 128),
+        in_specs=on_chip(5),
+        out_specs=on_chip(1)[0],
+        compiler_params=small(),
+        cost_estimate=pl.CostEstimate(flops=3_000_000_000, bytes_accessed=300_000, transcendentals=20_000),
+    )(*values)
+
+
+def drag_of(side, values, result):
+    blocks = values[1].shape[0]
+    in_hbm = pl.BlockSpec(memory_space=pltpu.HBM)
+    return pl.pallas_call(
+        functools.partial(drag_kernel, side),
+        out_shape=(array_of(cells_x, cells_y, cells_z), array_of(3, blocks, 128)),
+        in_specs=on_chip(2) + [in_hbm] + on_chip(6) + [in_hbm] * len(result),
+        out_specs=(in_hbm,) * 2,
+        scratch_shapes=[
+            pltpu.VMEM((cells_x, cells_y, cells_z), jnp.float32),
+            pltpu.VMEM((3, blocks, 128), jnp.float32),
+            pltpu.VMEM((3, blocks, 128), jnp.float32),
+            pltpu.SemaphoreType.DMA((3,)),
+        ],
+        input_output_aliases={9: 0, 10: 1} if result else {},
+        compiler_params=small(),
+    )(*values, *result)
+
+
 def small():
     return pltpu.CompilerParams(vmem_limit_bytes=16 * 1024 * 1024)
 
@@ -237,6 +294,7 @@
     cells = jnp.transpose(satellite_cells[0, 0], (1, 0, 2))
     volume = particle_volume[0, 0]
     particles = jnp.transpose(particle_velocity[0, 0], (1, 0, 2))
+    particles = pltpu.with_memory_space_constraint(particles, pltpu.HBM)
     blocks = volume.shape[0]
     tile, x_up, x_down, share = pl.pallas_call(
         deposit_kernel,
@@ -261,24 +319,16 @@
         compiler_params=small(),
         name="middle",
     )(tile, fluid_velocity, x_below, x_above)
-    y_below, y_above = both_ways(y_up, y_down, "gy")
-    sums = pl.pallas_call(
-        early_kernel,
-        out_shape=array_of(4, blocks, 128),
-        in_specs=on_chip(5),
-        out_specs=on_chip(1)[0],
-        compiler_params=small(),
-        cost_estimate=pl.CostEstimate(flops=3_000_000_000, bytes_accessed=300_000, transcendentals=20_000),
-        name="early",
-    )(cells, fluid_velocity, tile, x_below, x_above)
-    void, drag = pl.pallas_call(
-        drag_kernel,
-        out_shape=(array_of(cells_x, cells_y, cells_z), array_of(3, blocks, 128)),
-        in_specs=on_chip(9),
-        out_specs=tuple(on_chip(2)),
-        compiler_params=small(),
-        name="drag",
-    )(cells, share, particles, tile, y_up, y_down, y_below, y_above, sums)
+    below_even = one_way(y_up, "gy", 1, 1)
+    above_even = one_way(y_down, "gy", 1, -1)
+    early_in = (cells, fluid_velocity, tile, x_below, x_above)
+    sums_even = early(0, early_in)
+    below_odd = one_way(y_up, "gy", 0, 1)
+    above_odd = one_way(y_down, "gy", 0, -1)
+    sums_odd = early(1, early_in)
+    rest = (cells, share, particles, tile, y_up, y_down)
+    result = drag_of(0, rest + (below_even, above_even, sums_even), ())
+    void, drag = drag_of(1, rest + (below_odd, above_odd, sums_odd), result)
     return void, jnp.transpose(drag, (1, 0, 2))[None, None]
 
 

time: 38.2 us -> 45.6 us (1.19)
  the two profiles are of different devices: /device:TPU:6 before, /device:TPU:32 now
where the time goes in v3:
time: 45.6 us; the launch traced here: 45.2 us
  starting transfers between devices  33.6 us (74%)
  Pallas kernels  8.44 us (19%)
  waiting for transfers between devices  1.69 us (4%)
  between operations  1.44 us (3%)
    ppermute x4, starting transfers between devices, one_way(): lax.ppermute(value, axis, [(i, (i + step) % count) for i in range(count)...  24.1 us
    ppermute x1, starting transfers between devices, both_ways(): lax.ppermute(down, axis, [((i + 1) % count, i) for i in range(count)])  7.55 us
    pallas_call x2, Pallas kernels, early(): pl.pallas_call(functools.partial(early_kernel, side), out_shape=array_of(...  3.1 us
    pallas_call x1, Pallas kernels, body(): pl.pallas_call(deposit_kernel, out_shape=(array_of(tile_rows, 128), array...  2.87 us
    pallas_call x2, Pallas kernels, drag_of(): pl.pallas_call(functools.partial(drag_kernel, side), out_shape=(array_of(...  2.44 us
    ppermute x1, starting transfers between devices, both_ways(): below = lax.ppermute(up, axis, [(i, (i + 1) % count) for i in range(count)])  1.92 us
    ppermute x1, waiting for transfers between devices, both_ways(): lax.ppermute(down, axis, [((i + 1) % count, i) for i in range(count)])  1.68 us
  transfers between devices with their start and end apart: 6, of which 1 were waited for; matrix products, arithmetic and copies ran while one was open for 0% of the time, Pallas kernels for 12%

profile of v3, /device:TPU:32, one launch (start us, length us, event | category | flops | bytes accessed | tf_op | source)
XLA Modules:
  0.0 45.2 jit_solution(18110591514387330523)
XLA Ops:
  0.6 0.0 copy-start.1
  1.3 2.9 %deposit.1 = (f32[112,128]{1,0:T(8,128)S(1)}, f32[88,128]{1,0:T(8,128)S(1)}, f32[88,128]{1,0:T(8,128)S(1)}, f32[4,128]{1,0:T(4,128)S(1)}) custom-call(s32[1,1]{1,0:T(1,128)S(6)} %copy.11.live_ref, s32[29,4,128]{2,1,0:T(4,128)} %bitcast.10, f32[4,128]{1,0:T(4,128)} %bitcast.18, f32[3,4,16,128]{3,2,1,0:T(8,128)} %velocity_ref.7), custom_call_target="tpu_custom_call" | custom-call | tf_op jit(solution)/shard_map/deposit/pallas_call | solution.py:299
  4.2 1.9 %collective-permute-start = (f32[88,128]{1,0:T(8,128)S(1)}, f32[88,128]{1,0:T(8,128)S(1)}, u32[]{:S(2)}, u32[]{:S(2)}) collective-permute-start(f32[88,128]{1,0:T(8,128)S(1)} %get-tuple-element.15), channel_id=1, source_target_pairs={{0,8},{8,16},{16,24},{24,32},{32,40},{40,48},{48,56},{56,64},{64,7... | collective-permute-start | bytes 135176 | tf_op jit(solution)/shard_map/ppermute | solution.py:249
  6.1 7.5 %collective-permute-start.1 = (f32[88,128]{1,0:T(8,128)S(1)}, f32[88,128]{1,0:T(8,128)S(1)}, u32[]{:S(2)}, u32[]{:S(2)}) collective-permute-start(f32[88,128]{1,0:T(8,128)S(1)} %get-tuple-element.16), channel_id=1, source_target_pairs={{8,0},{16,8},{24,16},{32,24},{40,32},{48,40},{56,48},{64,56},{72,6... | collective-permute-start | bytes 135176 | tf_op jit(solution)/shard_map/ppermute | solution.py:250
  13.7 0.0 collective-permute-done.below_ref
  13.7 1.7 %collective-permute-done.1.above_ref = f32[88,128]{1,0:T(8,128)S(1)} collective-permute-done((f32[88,128]{1,0:T(8,128)S(1)}, f32[88,128]{1,0:T(8,128)S(1)}, u32[]{:S(2)}, u32[]{:S(2)}) %collective-permute-start.1) | collective-permute-done | bytes 45088 | tf_op jit(solution)/shard_map/ppermute | solution.py:250
  15.4 0.0 copy-done.1
  15.4 0.0 copy-start
  15.4 1.3 %collective-permute-start.4 = (f32[40,128]{1,0:T(8,128)S(1)}, f32[40,128]{1,0:T(8,128)S(1)}, u32[]{:S(2)}, u32[]{:S(2)}) collective-permute-start(f32[40,128]{1,0:T(8,128)S(1)} %get-tuple-element.18.refs_4_), channel_id=1, source_target_pairs={{1,2},{3,4},{5,6},{7,0},{9,10},{11,12},{13,14},{15,8},{17,18},{19,... | collective-permute-start | bytes 61448 | tf_op jit(solution)/shard_map/ppermute | solution.py:256
  16.7 10.9 %collective-permute-start.2 = (f32[40,128]{1,0:T(8,128)S(1)}, f32[40,128]{1,0:T(8,128)S(1)}, u32[]{:S(2)}, u32[]{:S(2)}) collective-permute-start(f32[40,128]{1,0:T(8,128)S(1)} %get-tuple-element.18.refs_4_), channel_id=1, source_target_pairs={{0,1},{2,3},{4,5},{6,7},{8,9},{10,11},{12,13},{14,15},{16,17},{18,... | collective-permute-start | bytes 61448 | tf_op jit(solution)/shard_map/ppermute | solution.py:256
  27.6 1.3 %collective-permute-start.5 = (f32[40,128]{1,0:T(8,128)S(1)}, f32[40,128]{1,0:T(8,128)S(1)}, u32[]{:S(2)}, u32[]{:S(2)}) collective-permute-start(f32[40,128]{1,0:T(8,128)S(1)} %get-tuple-element.19.refs_5_), channel_id=1, source_target_pairs={{1,0},{3,2},{5,4},{7,6},{9,8},{11,10},{13,12},{15,14},{17,16},{19,... | collective-permute-start | bytes 61448 | tf_op jit(solution)/shard_map/ppermute | solution.py:256
  28.9 10.6 %collective-permute-start.3 = (f32[40,128]{1,0:T(8,128)S(1)}, f32[40,128]{1,0:T(8,128)S(1)}, u32[]{:S(2)}, u32[]{:S(2)}) collective-permute-start(f32[40,128]{1,0:T(8,128)S(1)} %get-tuple-element.19.refs_5_), channel_id=1, source_target_pairs={{0,7},{2,1},{4,3},{6,5},{8,15},{10,9},{12,11},{14,13},{16,23},{18,... | collective-permute-start | bytes 61448 | tf_op jit(solution)/shard_map/ppermute | solution.py:256
  39.6 0.0 copy-done
  39.6 3.1 %shard_map.69.refs_8_ = f32[4,4,128]{2,1,0:T(4,128)S(1)} custom-call(s32[29,4,128]{2,1,0:T(4,128)S(1)} %bitcast.11, f32[3,4,16,128]{3,2,1,0:T(8,128)S(1)} %copy-done.1, f32[112,128]{1,0:T(8,128)S(1)} %get-tuple-element.17.tile_ref.refs_3_, f32[88,128]{1,0:T(8,128)S(1)} %collective-permute-done.below_ref, f32[88,128]{1,0:T(8,128)S(1)} %collective-permute-done.1.above_ref), custom_call_target="tpu_custom_call" | custom-call | flops 3000000000 | bytes 300000 | tf_op jit(solution)/shard_map/pallas_call | solution.py:260
  42.7 0.0 collective-permute-done.4.refs_6_
  42.7 0.0 collective-permute-done.5.refs_7_
  42.7 2.4 %shard_map.70 = (f32[4,16,128]{2,1,0:T(8,128)}, f32[3,4,128]{2,1,0:T(4,128)}) custom-call(s32[29,4,128]{2,1,0:T(4,128)S(1)} %bitcast.13, f32[4,128]{1,0:T(4,128)S(1)} %get-tuple-element.13.refs_1_, f32[3,4,128]{2,1,0:T(4,128)} %bitcast.15, f32[112,128]{1,0:T(8,128)S(1)} %get-tuple-element.17.tile_ref.refs_3_, f32[40,128]{1,0:T(8,128)S(1)} %get-tuple-element.18.refs_4_, ...), custom_call_target="tpu_custom_call" | custom-call | tf_op jit(solution)/shard_map/pallas_call | solution.py:273
  45.1 0.0 collective-permute-done.2.refs_6_
  45.1 0.0 collective-permute-done.3.refs_7_
  (3 shorter events, 0.1 us)
Async XLA Ops:
  0.6 14.7 %copy-start.1 = (f32[3,4,16,128]{3,2,1,0:T(8,128)S(1)}, f32[3,4,16,128]{3,2,1,0:T(8,128)}, u32[]{:S(2)}) copy-start(f32[3,4,16,128]{3,2,1,0:T(8,128)} %velocity_ref.7) | copy-start | bytes 294916
  4.2 9.5 %collective-permute-start = (f32[88,128]{1,0:T(8,128)S(1)}, f32[88,128]{1,0:T(8,128)S(1)}, u32[]{:S(2)}, u32[]{:S(2)}) collective-permute-start(f32[88,128]{1,0:T(8,128)S(1)} %get-tuple-element.15), channel_id=1, source_target_pairs={{0,8},{8,16},{16,24},{24,32},{32,40},{40,48},{48,56},{56,64},{64,7... | collective-permute-start | bytes 135176 | tf_op jit(solution)/shard_map/ppermute | solution.py:249
  6.1 9.2 %collective-permute-start.1 = (f32[88,128]{1,0:T(8,128)S(1)}, f32[88,128]{1,0:T(8,128)S(1)}, u32[]{:S(2)}, u32[]{:S(2)}) collective-permute-start(f32[88,128]{1,0:T(8,128)S(1)} %get-tuple-element.16), channel_id=1, source_target_pairs={{8,0},{16,8},{24,16},{32,24},{40,32},{48,40},{56,48},{64,56},{72,6... | collective-permute-start | bytes 135176 | tf_op jit(solution)/shard_map/ppermute | solution.py:250
  15.4 24.2 %copy-start = (s32[1,1,4,29,128]{4,2,3,1,0:T(4,128)S(1)}, s32[1,1,4,29,128]{4,2,3,1,0:T(4,128)}, u32[]{:S(2)}) copy-start(s32[1,1,4,29,128]{4,2,3,1,0:T(4,128)} %param.8) | copy-start | bytes 178180
  15.4 27.3 %collective-permute-start.4 = (f32[40,128]{1,0:T(8,128)S(1)}, f32[40,128]{1,0:T(8,128)S(1)}, u32[]{:S(2)}, u32[]{:S(2)}) collective-permute-start(f32[40,128]{1,0:T(8,128)S(1)} %get-tuple-element.18.refs_4_), channel_id=1, source_target_pairs={{1,2},{3,4},{5,6},{7,0},{9,10},{11,12},{13,14},{15,8},{17,18},{19,... | collective-permute-start | bytes 61448 | tf_op jit(solution)/shard_map/ppermute | solution.py:256
  16.7 28.4 %collective-permute-start.2 = (f32[40,128]{1,0:T(8,128)S(1)}, f32[40,128]{1,0:T(8,128)S(1)}, u32[]{:S(2)}, u32[]{:S(2)}) collective-permute-start(f32[40,128]{1,0:T(8,128)S(1)} %get-tuple-element.18.refs_4_), channel_id=1, source_target_pairs={{0,1},{2,3},{4,5},{6,7},{8,9},{10,11},{12,13},{14,15},{16,17},{18,... | collective-permute-start | bytes 61448 | tf_op jit(solution)/shard_map/ppermute | solution.py:256
  27.6 15.1 %collective-permute-start.5 = (f32[40,128]{1,0:T(8,128)S(1)}, f32[40,128]{1,0:T(8,128)S(1)}, u32[]{:S(2)}, u32[]{:S(2)}) collective-permute-start(f32[40,128]{1,0:T(8,128)S(1)} %get-tuple-element.19.refs_5_), channel_id=1, source_target_pairs={{1,0},{3,2},{5,4},{7,6},{9,8},{11,10},{13,12},{15,14},{17,16},{19,... | collective-permute-start | bytes 61448 | tf_op jit(solution)/shard_map/ppermute | solution.py:256
  28.9 16.2 %collective-permute-start.3 = (f32[40,128]{1,0:T(8,128)S(1)}, f32[40,128]{1,0:T(8,128)S(1)}, u32[]{:S(2)}, u32[]{:S(2)}) collective-permute-start(f32[40,128]{1,0:T(8,128)S(1)} %get-tuple-element.19.refs_5_), channel_id=1, source_target_pairs={{0,7},{2,1},{4,3},{6,5},{8,15},{10,9},{12,11},{14,13},{16,23},{18,... | collective-permute-start | bytes 61448 | tf_op jit(solution)/shard_map/ppermute | solution.py:256

commit v4 on v3

--- a/solution.py
+++ b/solution.py
@@ -20,6 +20,10 @@
 early_padded = 88
 tile_rows = 112
 x_rows, x_flow, y_rows, y_flow = 88, 40, 40, 16
+
+
+def on_side(axis, side):
+    return lax.rem(lax.axis_index(axis), 2) == side
 
 
 def split_cells(cells):
@@ -56,19 +60,22 @@
     return [every[at : at + 2] for at in range(0, points, 2)]
 
 
-def deposit_kernel(
-    live_ref, cells_ref, volume_ref, velocity_ref, tile_ref, up_ref, down_ref, share_ref, cells_in, volume_in, live_in, sems
-):
+def deposit_kernel(live_ref, cells_ref, volume_ref, velocity_ref, particle_ref, *refs):
+    tile_ref, odd_ref, even_ref, share_ref, particle_out, cells_in, volume_in, live_in, sems = refs
     points, blocks = cells_ref.shape[0], cells_ref.shape[1]
+    is_even = on_side("gx", 0)
+    odd_layer = jnp.where(is_even, 0, cells_x - 1)
+    even_layer = cells_x - 1 - odd_layer
     copies = [
         pltpu.make_async_copy(cells_ref, cells_in, sems.at[0]),
         pltpu.make_async_copy(volume_ref, volume_in, sems.at[1]),
         pltpu.make_async_copy(live_ref, live_in, sems.at[2]),
+        pltpu.make_async_copy(particle_ref, particle_out, sems.at[9]),
     ]
     for f in range(3):
         at = pl.ds(x_flow + cells_y * f, cells_y)
-        copies.append(pltpu.make_async_copy(velocity_ref.at[f, cells_x - 1], up_ref.at[at], sems.at[3 + f]))
-        copies.append(pltpu.make_async_copy(velocity_ref.at[f, 0], down_ref.at[at], sems.at[6 + f]))
+        copies.append(pltpu.make_async_copy(velocity_ref.at[f, odd_layer], odd_ref.at[at], sems.at[3 + f]))
+        copies.append(pltpu.make_async_copy(velocity_ref.at[f, even_layer], even_ref.at[at], sems.at[6 + f]))
     for copy in copies:
         copy.start()
     row_at = narrow(counted(tile_rows))
@@ -109,34 +116,46 @@
         tile += alive * (totals[b][:tile_rows] + totals[b][tile_rows:])
         share_ref[b : b + 1] = alive * share[b : b + 1]
     tile_ref[...] = tile
-    up_ref[0:28] = tile_ref[80:108]
-    down_ref[0:28] = tile_ref[24:52]
+    lower, upper = tile_ref[24:52], tile_ref[80:108]
+    odd_ref[0:28] = jnp.where(is_even, lower, upper)
+    even_ref[0:28] = jnp.where(is_even, upper, lower)
     for g in range(4):
-        up_ref[28 + 2 * g : 30 + 2 * g] = tile_ref[6 * g + 4 : 6 * g + 6]
-        down_ref[28 + 2 * g : 30 + 2 * g] = tile_ref[6 * g : 6 * g + 2]
-    up_ref[36:40] = jnp.zeros((4, 128), jnp.float32)
-    down_ref[36:40] = jnp.zeros((4, 128), jnp.float32)
+        lower, upper = tile_ref[6 * g : 6 * g + 2], tile_ref[6 * g + 4 : 6 * g + 6]
+        odd_ref[28 + 2 * g : 30 + 2 * g] = jnp.where(is_even, lower, upper)
+        even_ref[28 + 2 * g : 30 + 2 * g] = jnp.where(is_even, upper, lower)
+    odd_ref[36:40] = jnp.zeros((4, 128), jnp.float32)
+    even_ref[36:40] = jnp.zeros((4, 128), jnp.float32)
     for copy in copies[3:]:
         copy.wait()
 
 
-def middle_kernel(tile_ref, velocity_ref, below_ref, above_ref, out_ref, up_ref, down_ref):
+def middle_kernel(tile_ref, velocity_ref, odd_ref, even_ref, out_ref, up_ref, down_ref, flow_ref):
+    is_even = on_side("gx", 0)
+
+    def from_below(first, last):
+        return jnp.where(is_even, odd_ref[first:last], even_ref[first:last])
+
+    def from_above(first, last):
+        return jnp.where(is_even, even_ref[first:last], odd_ref[first:last])
+
     out_ref[...] = tile_ref[...]
-    out_ref[24:52] += below_ref[0:28]
-    out_ref[80:108] += above_ref[0:28]
+    out_ref[24:52] += from_below(0, 28)
+    out_ref[80:108] += from_above(0, 28)
     for g in range(4):
-        out_ref[6 * g : 6 * g + 2] += below_ref[28 + 2 * g : 30 + 2 * g]
-        out_ref[6 * g + 4 : 6 * g + 6] += above_ref[28 + 2 * g : 30 + 2 * g]
+        out_ref[6 * g : 6 * g + 2] += from_below(28 + 2 * g, 30 + 2 * g)
+        out_ref[6 * g + 4 : 6 * g + 6] += from_above(28 + 2 * g, 30 + 2 * g)
+    flow_ref[0:48] = from_below(x_flow, x_rows)
+    flow_ref[48:96] = from_above(x_flow, x_rows)
 
     def fill(dest_ref, first, near):
         dest_ref[...] = jnp.zeros((y_rows, 128), jnp.float32)
         dest_ref[0:12] = out_ref[first : first + 12]
         for f in range(3):
-            at, halo = y_flow + 8 * f, x_flow + cells_y * f + near
-            dest_ref[at : at + 1] = below_ref[halo : halo + 1]
+            at, halo = y_flow + 8 * f, cells_y * f + near
+            dest_ref[at : at + 1] = flow_ref[halo : halo + 1]
             for i in range(cells_x):
                 dest_ref[at + 1 + i : at + 2 + i] = velocity_ref[f, i, near : near + 1]
-            dest_ref[at + 5 : at + 6] = above_ref[halo : halo + 1]
+            dest_ref[at + 5 : at + 6] = flow_ref[48 + halo : 49 + halo]
 
     fill(up_ref, 12, cells_y - 1)
     fill(down_ref, 0, 0)
@@ -176,20 +195,16 @@
     return jnp.exp(exponent * jnp.log(void))
 
 
-def on_side(side):
-    return lax.rem(lax.axis_index("gy"), 2) == side
-
-
-def early_kernel(side, cells_ref, velocity_ref, tile_ref, below_ref, above_ref, sums_ref):
-    @pl.when(on_side(side))
+def early_kernel(side, cells_ref, velocity_ref, tile_ref, flow_ref, sums_ref):
+    @pl.when(on_side("gy", side))
     def _():
         resistance = resistance_of(void_of(tile_ref[late_rows : late_rows + early_rows]))
         fields = [resistance]
         for f in range(3):
-            halo = x_flow + cells_y * f + 1
-            flow = [below_ref[halo : halo + own_y]]
+            halo = cells_y * f + 1
+            flow = [flow_ref[halo : halo + own_y]]
             flow += [velocity_ref[f, i, 1 : 1 + own_y] for i in range(cells_x)]
-            flow += [above_ref[halo : halo + own_y]]
+            flow += [flow_ref[48 + halo : 48 + halo + own_y]]
             fields.append(resistance * jnp.concatenate(flow, axis=0))
         blank = jnp.zeros((early_padded - early_rows, 128), jnp.float32)
         fields = [jnp.concatenate([field, blank], axis=0) for field in fields]
@@ -200,12 +215,10 @@
 
 def drag_kernel(side, *refs):
     cells_ref, share_ref, particle_ref, tile_ref, up_ref, down_ref, below_ref, above_ref, sums_ref = refs[:9]
-    void_out, drag_out, void_ref, drag_ref, particle_in, sems = refs[-6:]
-
-    @pl.when(on_side(side))
+    void_out, drag_out, void_ref, drag_ref, sems = refs[-5:]
+
+    @pl.when(on_side("gy", side))
     def _():
-        fetch = pltpu.make_async_copy(particle_ref, particle_in, sems.at[2])
-        fetch.start()
         late = jnp.concatenate([tile_ref[0:12] + below_ref[0:12], tile_ref[12:24] + above_ref[0:12]], axis=0)
         late_void = void_of(late)
         early_void = void_of(tile_ref[late_rows : late_rows + early_rows])
@@ -219,12 +232,10 @@
             at = slice(y_flow + 8 * f, y_flow + 8 * f + wide_x)
             flow = jnp.concatenate([below_ref[at], down_ref[at], up_ref[at], above_ref[at]], axis=0)
             fields.append(resistance * flow)
-        found = looked_up(cells_ref, fields, 0)
-        fetch.wait()
-        for b, sums in enumerate(found):
+        for b, sums in enumerate(looked_up(cells_ref, fields, 0)):
             total = [sums[f] + sums_ref[f, b : b + 1] for f in range(4)]
             for f in range(3):
-                force = total[f + 1] - particle_in[f, b : b + 1] * total[0]
+                force = total[f + 1] - particle_ref[f, b : b + 1] * total[0]
                 drag_ref[f, b : b + 1] = drag_scale * share_ref[b : b + 1] * force
         copies = [
             pltpu.make_async_copy(void_ref, void_out, sems.at[0]),
@@ -244,11 +255,9 @@
     return jax.ShapeDtypeStruct(shape, jnp.float32)
 
 
-def both_ways(up, down, axis):
+def swapped(value, axis, odd):
     count = lax.axis_size(axis)
-    below = lax.ppermute(up, axis, [(i, (i + 1) % count) for i in range(count)])
-    above = lax.ppermute(down, axis, [((i + 1) % count, i) for i in range(count)])
-    return below, above
+    return lax.ppermute(value, axis, [(i, (i + 1 if i % 2 == odd else i - 1) % count) for i in range(count)])
 
 
 def one_way(value, axis, side, step):
@@ -260,7 +269,7 @@
     return pl.pallas_call(
         functools.partial(early_kernel, side),
         out_shape=array_of(4, values[0].shape[1], 128),
-        in_specs=on_chip(5),
+        in_specs=on_chip(4),
         out_specs=on_chip(1)[0],
         compiler_params=small(),
         cost_estimate=pl.CostEstimate(flops=3_000_000_000, bytes_accessed=300_000, transcendentals=20_000),
@@ -273,13 +282,12 @@
     return pl.pallas_call(
         functools.partial(drag_kernel, side),
         out_shape=(array_of(cells_x, cells_y, cells_z), array_of(3, blocks, 128)),
-        in_specs=on_chip(2) + [in_hbm] + on_chip(6) + [in_hbm] * len(result),
+        in_specs=on_chip(9) + [in_hbm] * len(result),
         out_specs=(in_hbm,) * 2,
         scratch_shapes=[
             pltpu.VMEM((cells_x, cells_y, cells_z), jnp.float32),
             pltpu.VMEM((3, blocks, 128), jnp.float32),
-            pltpu.VMEM((3, blocks, 128), jnp.float32),
-            pltpu.SemaphoreType.DMA((3,)),
+            pltpu.SemaphoreType.DMA((2,)),
         ],
         input_output_aliases={9: 0, 10: 1} if result else {},
         compiler_params=small(),
@@ -294,34 +302,34 @@
     cells = jnp.transpose(satellite_cells[0, 0], (1, 0, 2))
     volume = particle_volume[0, 0]
     particles = jnp.transpose(particle_velocity[0, 0], (1, 0, 2))
-    particles = pltpu.with_memory_space_constraint(particles, pltpu.HBM)
     blocks = volume.shape[0]
-    tile, x_up, x_down, share = pl.pallas_call(
+    tile, x_odd, x_even, share, particles = pl.pallas_call(
         deposit_kernel,
-        out_shape=(array_of(tile_rows, 128), array_of(x_rows, 128), array_of(x_rows, 128), array_of(blocks, 128)),
-        in_specs=[pl.BlockSpec(memory_space=pltpu.HBM)] * 4,
-        out_specs=tuple(on_chip(4)),
+        out_shape=(array_of(tile_rows, 128), array_of(x_rows, 128), array_of(x_rows, 128), array_of(blocks, 128), array_of(3, blocks, 128)),
+        in_specs=[pl.BlockSpec(memory_space=pltpu.HBM)] * 5,
+        out_specs=tuple(on_chip(5)),
         scratch_shapes=[
             pltpu.VMEM(cells.shape, jnp.int32),
             pltpu.VMEM(volume.shape, jnp.float32),
             pltpu.SMEM(live_blocks.shape, jnp.int32),
-            pltpu.SemaphoreType.DMA((9,)),
+            pltpu.SemaphoreType.DMA((10,)),
         ],
         compiler_params=small(),
         name="deposit",
-    )(live_blocks, *(pltpu.with_memory_space_constraint(value, pltpu.HBM) for value in (cells, volume, fluid_velocity)))
-    x_below, x_above = both_ways(x_up, x_down, "gx")
-    tile, y_up, y_down = pl.pallas_call(
+    )(live_blocks, *(pltpu.with_memory_space_constraint(value, pltpu.HBM) for value in (cells, volume, fluid_velocity, particles)))
+    x_odd = swapped(x_odd, "gx", 1)
+    x_even = swapped(x_even, "gx", 0)
+    tile, y_up, y_down, flow = pl.pallas_call(
         middle_kernel,
-        out_shape=(array_of(tile_rows, 128), array_of(y_rows, 128), array_of(y_rows, 128)),
+        out_shape=(array_of(tile_rows, 128), array_of(y_rows, 128), array_of(y_rows, 128), array_of(96, 128)),
         in_specs=on_chip(4),
-        out_specs=tuple(on_chip(3)),
+        out_specs=tuple(on_chip(4)),
         compiler_params=small(),
         name="middle",
-    )(tile, fluid_velocity, x_below, x_above)
+    )(tile, fluid_velocity, x_odd, x_even)
     below_even = one_way(y_up, "gy", 1, 1)
     above_even = one_way(y_down, "gy", 1, -1)
-    early_in = (cells, fluid_velocity, tile, x_below, x_above)
+    early_in = (cells, fluid_velocity, tile, flow)
     sums_even = early(0, early_in)
     below_odd = one_way(y_up, "gy", 0, 1)
     above_odd = one_way(y_down, "gy", 0, -1)

time: 45.6 us -> 44.9 us (0.985)
  the two profiles are of different devices: /device:TPU:32 before, /device:TPU:1 now
where the time goes in v4:
time: 44.9 us; the launch traced here: 44.6 us
  starting transfers between devices  34.2 us (76%)
  Pallas kernels  8.05 us (18%)
  between operations  1.44 us (3%)
  waiting for transfers between devices  0.86 us (2%)
    ppermute x4, starting transfers between devices, one_way(): lax.ppermute(value, axis, [(i, (i + step) % count) for i in range(count)...  20.6 us
    ppermute x2, starting transfers between devices, swapped(): lax.ppermute(value, axis, [(i, (i + 1 if i % 2 == odd else i - 1) % count...  13.6 us
    pallas_call x2, Pallas kernels, early(): pl.pallas_call(functools.partial(early_kernel, side), out_shape=array_of(...  3.1 us
    pallas_call x1, Pallas kernels, body(): pl.pallas_call(deposit_kernel, out_shape=(array_of(tile_rows, 128), array...  2.88 us
    pallas_call x2, Pallas kernels, drag_of(): pl.pallas_call(functools.partial(drag_kernel, side), out_shape=(array_of(...  2.03 us
  transfers between devices with their start and end apart: 6, of which 1 were waited for; matrix products, arithmetic and copies ran while one was open for 0% of the time, Pallas kernels for 11%

profile of v4, /device:TPU:1, one launch (start us, length us, event | category | flops | bytes accessed | tf_op | source)
XLA Modules:
  0.0 44.6 jit_solution(8075960034792848998)
XLA Ops:
  0.6 0.0 copy-start.1
  1.3 2.9 %deposit.1 = (f32[112,128]{1,0:T(8,128)S(1)}, f32[88,128]{1,0:T(8,128)S(1)}, f32[88,128]{1,0:T(8,128)S(1)}, f32[4,128]{1,0:T(4,128)S(1)}, f32[3,4,128]{2,1,0:T(4,128)S(1)}) custom-call(s32[1,1]{1,0:T(1,128)S(6)} %copy.11.live_ref, s32[29,4,128]{2,1,0:T(4,128)} %bitcast.10, f32[4,128]{1,0:T(4,128)} %bitcast.17, f32[3,4,16,128]{3,2,1,0:T(8,128)} %velocity_ref.7, ...), custom_call_target="tpu_custom_call" | custom-call | tf_op jit(solution)/shard_map/deposit/pallas_call | solution.py:306
  4.2 5.4 %collective-permute-start = (f32[88,128]{1,0:T(8,128)S(1)}, f32[88,128]{1,0:T(8,128)S(1)}, u32[]{:S(2)}, u32[]{:S(2)}) collective-permute-start(f32[88,128]{1,0:T(8,128)S(1)} %get-tuple-element.18), channel_id=1, source_target_pairs={{0,504},{8,16},{16,8},{24,32},{32,24},{40,48},{48,40},{56,64},{64,... | collective-permute-start | bytes 135176 | tf_op jit(solution)/shard_map/ppermute | solution.py:260
  9.6 8.3 %collective-permute-start.1 = (f32[88,128]{1,0:T(8,128)S(1)}, f32[88,128]{1,0:T(8,128)S(1)}, u32[]{:S(2)}, u32[]{:S(2)}) collective-permute-start(f32[88,128]{1,0:T(8,128)S(1)} %get-tuple-element.19), channel_id=1, source_target_pairs={{0,8},{8,0},{16,24},{24,16},{32,40},{40,32},{48,56},{56,48},{64,72... | collective-permute-start | bytes 135176 | tf_op jit(solution)/shard_map/ppermute | solution.py:260
  17.9 0.0 collective-permute-done.odd_ref
  17.9 0.8 %collective-permute-done.1.even_ref = f32[88,128]{1,0:T(8,128)S(1)} collective-permute-done((f32[88,128]{1,0:T(8,128)S(1)}, f32[88,128]{1,0:T(8,128)S(1)}, u32[]{:S(2)}, u32[]{:S(2)}) %collective-permute-start.1) | collective-permute-done | bytes 45088 | tf_op jit(solution)/shard_map/ppermute | solution.py:260
  18.7 0.0 copy-done.1
  18.7 0.0 copy-start
  18.8 1.3 %collective-permute-start.4 = (f32[40,128]{1,0:T(8,128)S(1)}, f32[40,128]{1,0:T(8,128)S(1)}, u32[]{:S(2)}, u32[]{:S(2)}) collective-permute-start(f32[40,128]{1,0:T(8,128)S(1)} %get-tuple-element.21.refs_4_), channel_id=1, source_target_pairs={{1,2},{3,4},{5,6},{7,0},{9,10},{11,12},{13,14},{15,8},{17,18},{19,... | collective-permute-start | bytes 61448 | tf_op jit(solution)/shard_map/ppermute | solution.py:265
  20.1 8.8 %collective-permute-start.2 = (f32[40,128]{1,0:T(8,128)S(1)}, f32[40,128]{1,0:T(8,128)S(1)}, u32[]{:S(2)}, u32[]{:S(2)}) collective-permute-start(f32[40,128]{1,0:T(8,128)S(1)} %get-tuple-element.21.refs_4_), channel_id=1, source_target_pairs={{0,1},{2,3},{4,5},{6,7},{8,9},{10,11},{12,13},{14,15},{16,17},{18,... | collective-permute-start | bytes 61448 | tf_op jit(solution)/shard_map/ppermute | solution.py:265
  28.9 1.3 %collective-permute-start.5 = (f32[40,128]{1,0:T(8,128)S(1)}, f32[40,128]{1,0:T(8,128)S(1)}, u32[]{:S(2)}, u32[]{:S(2)}) collective-permute-start(f32[40,128]{1,0:T(8,128)S(1)} %get-tuple-element.22.refs_5_), channel_id=1, source_target_pairs={{1,0},{3,2},{5,4},{7,6},{9,8},{11,10},{13,12},{15,14},{17,16},{19,... | collective-permute-start | bytes 61448 | tf_op jit(solution)/shard_map/ppermute | solution.py:265
  30.2 9.2 %collective-permute-start.3 = (f32[40,128]{1,0:T(8,128)S(1)}, f32[40,128]{1,0:T(8,128)S(1)}, u32[]{:S(2)}, u32[]{:S(2)}) collective-permute-start(f32[40,128]{1,0:T(8,128)S(1)} %get-tuple-element.22.refs_5_), channel_id=1, source_target_pairs={{0,7},{2,1},{4,3},{6,5},{8,15},{10,9},{12,11},{14,13},{16,23},{18,... | collective-permute-start | bytes 61448 | tf_op jit(solution)/shard_map/ppermute | solution.py:265
  39.4 0.0 copy-done
  39.4 3.1 %shard_map.69.refs_8_ = f32[4,4,128]{2,1,0:T(4,128)S(1)} custom-call(s32[29,4,128]{2,1,0:T(4,128)S(1)} %bitcast.11, f32[3,4,16,128]{3,2,1,0:T(8,128)S(1)} %copy-done.1, f32[112,128]{1,0:T(8,128)S(1)} %get-tuple-element.20.tile_ref.refs_3_, f32[96,128]{1,0:T(8,128)S(1)} %get-tuple-element.23.flow_ref), custom_call_target="tpu_custom_call" | custom-call | flops 3000000000 | bytes 300000 | tf_op jit(solution)/shard_map/pallas_call | solution.py:269
  42.5 0.0 collective-permute-done.4.refs_6_
  42.5 0.0 collective-permute-done.5.refs_7_
  42.5 2.0 %shard_map.70 = (f32[4,16,128]{2,1,0:T(8,128)}, f32[3,4,128]{2,1,0:T(4,128)}) custom-call(s32[29,4,128]{2,1,0:T(4,128)S(1)} %bitcast.13, f32[4,128]{1,0:T(4,128)S(1)} %get-tuple-element.15.refs_1_, f32[3,4,128]{2,1,0:T(4,128)S(1)} %get-tuple-element.16.refs_2_, f32[112,128]{1,0:T(8,128)S(1)} %get-tuple-element.20.tile_ref.refs_3_, ...), custom_call_target="tpu_custom_call" | custom-call | tf_op jit(solution)/shard_map/pallas_call | solution.py:282
  44.5 0.0 collective-permute-done.2.refs_6_
  44.6 0.0 collective-permute-done.3.refs_7_
  (3 shorter events, 0.1 us)
Async XLA Ops:
  0.6 18.1 %copy-start.1 = (f32[3,4,16,128]{3,2,1,0:T(8,128)S(1)}, f32[3,4,16,128]{3,2,1,0:T(8,128)}, u32[]{:S(2)}) copy-start(f32[3,4,16,128]{3,2,1,0:T(8,128)} %velocity_ref.7) | copy-start | bytes 294916
  4.2 13.7 %collective-permute-start = (f32[88,128]{1,0:T(8,128)S(1)}, f32[88,128]{1,0:T(8,128)S(1)}, u32[]{:S(2)}, u32[]{:S(2)}) collective-permute-start(f32[88,128]{1,0:T(8,128)S(1)} %get-tuple-element.18), channel_id=1, source_target_pairs={{0,504},{8,16},{16,8},{24,32},{32,24},{40,48},{48,40},{56,64},{64,... | collective-permute-start | bytes 135176 | tf_op jit(solution)/shard_map/ppermute | solution.py:260
  9.6 9.1 %collective-permute-start.1 = (f32[88,128]{1,0:T(8,128)S(1)}, f32[88,128]{1,0:T(8,128)S(1)}, u32[]{:S(2)}, u32[]{:S(2)}) collective-permute-start(f32[88,128]{1,0:T(8,128)S(1)} %get-tuple-element.19), channel_id=1, source_target_pairs={{0,8},{8,0},{16,24},{24,16},{32,40},{40,32},{48,56},{56,48},{64,72... | collective-permute-start | bytes 135176 | tf_op jit(solution)/shard_map/ppermute | solution.py:260
  18.7 20.7 %copy-start = (s32[1,1,4,29,128]{4,2,3,1,0:T(4,128)S(1)}, s32[1,1,4,29,128]{4,2,3,1,0:T(4,128)}, u32[]{:S(2)}) copy-start(s32[1,1,4,29,128]{4,2,3,1,0:T(4,128)} %param.8) | copy-start | bytes 178180
  18.8 23.8 %collective-permute-start.4 = (f32[40,128]{1,0:T(8,128)S(1)}, f32[40,128]{1,0:T(8,128)S(1)}, u32[]{:S(2)}, u32[]{:S(2)}) collective-permute-start(f32[40,128]{1,0:T(8,128)S(1)} %get-tuple-element.21.refs_4_), channel_id=1, source_target_pairs={{1,2},{3,4},{5,6},{7,0},{9,10},{11,12},{13,14},{15,8},{17,18},{19,... | collective-permute-start | bytes 61448 | tf_op jit(solution)/shard_map/ppermute | solution.py:265
  20.1 24.5 %collective-permute-start.2 = (f32[40,128]{1,0:T(8,128)S(1)}, f32[40,128]{1,0:T(8,128)S(1)}, u32[]{:S(2)}, u32[]{:S(2)}) collective-permute-start(f32[40,128]{1,0:T(8,128)S(1)} %get-tuple-element.21.refs_4_), channel_id=1, source_target_pairs={{0,1},{2,3},{4,5},{6,7},{8,9},{10,11},{12,13},{14,15},{16,17},{18,... | collective-permute-start | bytes 61448 | tf_op jit(solution)/shard_map/ppermute | solution.py:265
  28.9 13.6 %collective-permute-start.5 = (f32[40,128]{1,0:T(8,128)S(1)}, f32[40,128]{1,0:T(8,128)S(1)}, u32[]{:S(2)}, u32[]{:S(2)}) collective-permute-start(f32[40,128]{1,0:T(8,128)S(1)} %get-tuple-element.22.refs_5_), channel_id=1, source_target_pairs={{1,0},{3,2},{5,4},{7,6},{9,8},{11,10},{13,12},{15,14},{17,16},{19,... | collective-permute-start | bytes 61448 | tf_op jit(solution)/shard_map/ppermute | solution.py:265
  30.2 14.4 %collective-permute-start.3 = (f32[40,128]{1,0:T(8,128)S(1)}, f32[40,128]{1,0:T(8,128)S(1)}, u32[]{:S(2)}, u32[]{:S(2)}) collective-permute-start(f32[40,128]{1,0:T(8,128)S(1)} %get-tuple-element.22.refs_5_), channel_id=1, source_target_pairs={{0,7},{2,1},{4,3},{6,5},{8,15},{10,9},{12,11},{14,13},{16,23},{18,... | collective-permute-start | bytes 61448 | tf_op jit(solution)/shard_map/ppermute | solution.py:265

commit v5 on v4

--- a/solution.py
+++ b/solution.py
@@ -26,11 +26,15 @@
     return lax.rem(lax.axis_index(axis), 2) == side
 
 
-def split_cells(cells):
+def columns_of(cells):
     lane = cells & (cells_z - 1)
     column = cells >> 7
     i = (column * 3641) >> 16
-    j = column - i * wide_y
+    return i, column - i * wide_y, lane
+
+
+def split_cells(cells):
+    i, j, lane = columns_of(cells)
     late = jnp.where(j < 2, j, j - own_y) * wide_x + i
     early = late_rows + i * own_y + (j - 2)
     row = jnp.where((j < 2) | (j >= wide_y - 2), late, early)
@@ -60,37 +64,16 @@
     return [every[at : at + 2] for at in range(0, points, 2)]
 
 
-def deposit_kernel(live_ref, cells_ref, volume_ref, velocity_ref, particle_ref, *refs):
-    tile_ref, odd_ref, even_ref, share_ref, particle_out, cells_in, volume_in, live_in, sems = refs
+def deposited(cells_ref, high, low, row_of, rows):
     points, blocks = cells_ref.shape[0], cells_ref.shape[1]
-    is_even = on_side("gx", 0)
-    odd_layer = jnp.where(is_even, 0, cells_x - 1)
-    even_layer = cells_x - 1 - odd_layer
-    copies = [
-        pltpu.make_async_copy(cells_ref, cells_in, sems.at[0]),
-        pltpu.make_async_copy(volume_ref, volume_in, sems.at[1]),
-        pltpu.make_async_copy(live_ref, live_in, sems.at[2]),
-        pltpu.make_async_copy(particle_ref, particle_out, sems.at[9]),
-    ]
-    for f in range(3):
-        at = pl.ds(x_flow + cells_y * f, cells_y)
-        copies.append(pltpu.make_async_copy(velocity_ref.at[f, odd_layer], odd_ref.at[at], sems.at[3 + f]))
-        copies.append(pltpu.make_async_copy(velocity_ref.at[f, even_layer], even_ref.at[at], sems.at[6 + f]))
-    for copy in copies:
-        copy.start()
-    row_at = narrow(counted(tile_rows))
+    row_at = narrow(counted(rows))
     lane_at = narrow(counted(cells_z))
     one = jnp.ones((), jnp.bfloat16)
     zero = jnp.zeros((), jnp.bfloat16)
-    copies[1].wait()
-    share = volume_in[...] / points
-    high, low = halves(share)
-    copies[0].wait()
-    totals = []
+    total = jnp.zeros((2 * rows, cells_z), jnp.float32)
     for b in range(blocks):
-        row, lane = split_cells(points_in(cells_in, b))
-        row, lane = narrow(row), narrow(lane)
-        total = jnp.zeros((2 * tile_rows, cells_z), jnp.float32)
+        i, j, lane = columns_of(points_in(cells_ref, b))
+        row, lane = narrow(row_of(i, j)), narrow(lane)
         for pair in pairs_of(b, points):
             left, right = [], []
             for _, s in pair:
@@ -107,29 +90,66 @@
                 (((1,), (1,)), ((), ())),
                 preferred_element_type=jnp.float32,
             )
-        totals.append(total)
-    copies[2].wait()
-    live = live_in[0, 0]
-    tile = jnp.zeros((tile_rows, cells_z), jnp.float32)
+    return total[:rows] + total[rows:]
+
+
+def layer_row(i, j):
+    early = i * own_y + j - 2
+    late = 2 * own_y + jnp.where(j < 2, j, j - own_y) * 2 + i
+    return jnp.where(is_late(j), late, early)
+
+
+def is_late(j):
+    return (j < 2) | (j >= wide_y - 2)
+
+
+def outer_row(i, j):
+    upper = i >= cells_x
+    row = layer_row(jnp.where(upper, i - cells_x, i), j) + jnp.where(upper, 36, 0)
+    inner = jnp.where(is_late(j), layer_row(i - 2, j) + 44, 127)
+    return jnp.where((i == 2) | (i == 3), inner, row)
+
+
+def inner_row(i, j):
+    return jnp.where(((i == 2) | (i == 3)) & ~is_late(j), layer_row(i - 2, j), 127)
+
+
+def deposit_kernel(live_ref, cells_ref, volume_ref, velocity_ref, particle_ref, *refs):
+    odd_ref, even_ref, late_ref, share_ref, particle_out, cells_in, volume_in, sems = refs
+    points, blocks = cells_ref.shape[0], cells_ref.shape[1]
+    is_even = on_side("gx", 0)
+    odd_layer = jnp.where(is_even, 0, cells_x - 1)
+    even_layer = cells_x - 1 - odd_layer
+    copies = [
+        pltpu.make_async_copy(cells_ref, cells_in, sems.at[0]),
+        pltpu.make_async_copy(volume_ref, volume_in, sems.at[1]),
+        pltpu.make_async_copy(particle_ref, particle_out, sems.at[2]),
+    ]
+    for f in range(3):
+        at = pl.ds(x_flow + cells_y * f, cells_y)
+        copies.append(pltpu.make_async_copy(velocity_ref.at[f, odd_layer], odd_ref.at[at], sems.at[3 + f]))
+        copies.append(pltpu.make_async_copy(velocity_ref.at[f, even_layer], even_ref.at[at], sems.at[6 + f]))
+    for copy in copies:
+        copy.start()
+    live = live_ref[0, 0]
+    copies[1].wait()
     for b in range(blocks):
-        alive = jnp.where(b < live, 1.0, 0.0)
-        tile += alive * (totals[b][:tile_rows] + totals[b][tile_rows:])
-        share_ref[b : b + 1] = alive * share[b : b + 1]
-    tile_ref[...] = tile
-    lower, upper = tile_ref[24:52], tile_ref[80:108]
-    odd_ref[0:28] = jnp.where(is_even, lower, upper)
-    even_ref[0:28] = jnp.where(is_even, upper, lower)
-    for g in range(4):
-        lower, upper = tile_ref[6 * g : 6 * g + 2], tile_ref[6 * g + 4 : 6 * g + 6]
-        odd_ref[28 + 2 * g : 30 + 2 * g] = jnp.where(is_even, lower, upper)
-        even_ref[28 + 2 * g : 30 + 2 * g] = jnp.where(is_even, upper, lower)
+        share_ref[b : b + 1] = jnp.where(b < live, 1.0, 0.0) * volume_in[b : b + 1] / points
+    copies[0].wait()
+    high, low = halves(share_ref[...])
+    total = deposited(cells_in, high, low, outer_row, 80)
+    late_ref[...] = total[72:80]
+    lower, upper = total[0:36], total[36:72]
+    odd_ref[0:36] = jnp.where(is_even, lower, upper)
+    even_ref[0:36] = jnp.where(is_even, upper, lower)
     odd_ref[36:40] = jnp.zeros((4, 128), jnp.float32)
     even_ref[36:40] = jnp.zeros((4, 128), jnp.float32)
-    for copy in copies[3:]:
+    for copy in copies[2:]:
         copy.wait()
 
 
-def middle_kernel(tile_ref, velocity_ref, odd_ref, even_ref, out_ref, up_ref, down_ref, flow_ref):
+def middle_kernel(late_ref, velocity_ref, *refs):
+    sent_odd_ref, sent_even_ref, odd_ref, even_ref, out_ref, up_ref, down_ref, flow_ref = refs
     is_even = on_side("gx", 0)
 
     def from_below(first, last):
@@ -138,12 +158,21 @@
     def from_above(first, last):
         return jnp.where(is_even, even_ref[first:last], odd_ref[first:last])
 
-    out_ref[...] = tile_ref[...]
-    out_ref[24:52] += from_below(0, 28)
-    out_ref[80:108] += from_above(0, 28)
+    def all_lower(first, last):
+        return jnp.where(is_even, sent_odd_ref[first:last], sent_even_ref[first:last]) + from_below(first, last)
+
+    def all_upper(first, last):
+        return jnp.where(is_even, sent_even_ref[first:last], sent_odd_ref[first:last]) + from_above(first, last)
+
+    out_ref[24:52] = all_lower(0, 28)
+    out_ref[52:80] = jnp.zeros((28, 128), jnp.float32)
+    out_ref[80:108] = all_upper(0, 28)
+    out_ref[108:112] = jnp.zeros((4, 128), jnp.float32)
     for g in range(4):
-        out_ref[6 * g : 6 * g + 2] += from_below(28 + 2 * g, 30 + 2 * g)
-        out_ref[6 * g + 4 : 6 * g + 6] += from_above(28 + 2 * g, 30 + 2 * g)
+        at = slice(28 + 2 * g, 30 + 2 * g)
+        out_ref[6 * g : 6 * g + 2] = all_lower(at.start, at.stop)
+        out_ref[6 * g + 2 : 6 * g + 4] = late_ref[2 * g : 2 * g + 2]
+        out_ref[6 * g + 4 : 6 * g + 6] = all_upper(at.start, at.stop)
     flow_ref[0:48] = from_below(x_flow, x_rows)
     flow_ref[48:96] = from_above(x_flow, x_rows)
 
@@ -195,10 +224,16 @@
     return jnp.exp(exponent * jnp.log(void))
 
 
-def early_kernel(side, cells_ref, velocity_ref, tile_ref, flow_ref, sums_ref):
+def early_void_of(tile_ref, inner_ref):
+    return void_of(jnp.concatenate([tile_ref[24:52], inner_ref[0:28], tile_ref[80:108]], axis=0))
+
+
+def early_kernel(side, cells_ref, share_ref, velocity_ref, tile_ref, flow_ref, sums_ref, inner_ref):
     @pl.when(on_side("gy", side))
     def _():
-        resistance = resistance_of(void_of(tile_ref[late_rows : late_rows + early_rows]))
+        high, low = halves(share_ref[...])
+        inner_ref[...] = deposited(cells_ref, high, low, inner_row, 32)
+        resistance = resistance_of(early_void_of(tile_ref, inner_ref))
         fields = [resistance]
         for f in range(3):
             halo = cells_y * f + 1
@@ -214,14 +249,14 @@
 
 
 def drag_kernel(side, *refs):
-    cells_ref, share_ref, particle_ref, tile_ref, up_ref, down_ref, below_ref, above_ref, sums_ref = refs[:9]
+    cells_ref, share_ref, particle_ref, tile_ref, up_ref, down_ref, below_ref, above_ref, sums_ref, inner_ref = refs[:10]
     void_out, drag_out, void_ref, drag_ref, sems = refs[-5:]
 
     @pl.when(on_side("gy", side))
     def _():
         late = jnp.concatenate([tile_ref[0:12] + below_ref[0:12], tile_ref[12:24] + above_ref[0:12]], axis=0)
         late_void = void_of(late)
-        early_void = void_of(tile_ref[late_rows : late_rows + early_rows])
+        early_void = early_void_of(tile_ref, inner_ref)
         for i in range(1, cells_x + 1):
             void_ref[i - 1, 0:1] = late_void[wide_x + i : wide_x + i + 1]
             void_ref[i - 1, 1 : 1 + own_y] = early_void[i * own_y : (i + 1) * own_y]
@@ -268,9 +303,9 @@
 def early(side, values):
     return pl.pallas_call(
         functools.partial(early_kernel, side),
-        out_shape=array_of(4, values[0].shape[1], 128),
-        in_specs=on_chip(4),
-        out_specs=on_chip(1)[0],
+        out_shape=(array_of(4, values[0].shape[1], 128), array_of(32, 128)),
+        in_specs=on_chip(5),
+        out_specs=tuple(on_chip(2)),
         compiler_params=small(),
         cost_estimate=pl.CostEstimate(flops=3_000_000_000, bytes_accessed=300_000, transcendentals=20_000),
     )(*values)
@@ -282,14 +317,14 @@
     return pl.pallas_call(
         functools.partial(drag_kernel, side),
         out_shape=(array_of(cells_x, cells_y, cells_z), array_of(3, blocks, 128)),
-        in_specs=on_chip(9) + [in_hbm] * len(result),
+        in_specs=on_chip(10) + [in_hbm] * len(result),
         out_specs=(in_hbm,) * 2,
         scratch_shapes=[
             pltpu.VMEM((cells_x, cells_y, cells_z), jnp.float32),
             pltpu.VMEM((3, blocks, 128), jnp.float32),
             pltpu.SemaphoreType.DMA((2,)),
         ],
-        input_output_aliases={9: 0, 10: 1} if result else {},
+        input_output_aliases={10: 0, 11: 1} if result else {},
         compiler_params=small(),
     )(*values, *result)
 
@@ -303,40 +338,40 @@
     volume = particle_volume[0, 0]
     particles = jnp.transpose(particle_velocity[0, 0], (1, 0, 2))
     blocks = volume.shape[0]
-    tile, x_odd, x_even, share, particles = pl.pallas_call(
+    fetched = (pltpu.with_memory_space_constraint(value, pltpu.HBM) for value in (cells, volume, fluid_velocity, particles))
+    x_odd, x_even, late, share, particles = pl.pallas_call(
         deposit_kernel,
-        out_shape=(array_of(tile_rows, 128), array_of(x_rows, 128), array_of(x_rows, 128), array_of(blocks, 128), array_of(3, blocks, 128)),
-        in_specs=[pl.BlockSpec(memory_space=pltpu.HBM)] * 5,
+        out_shape=tuple(array_of(rows, 128) for rows in (x_rows, x_rows, 8, blocks)) + (array_of(3, blocks, 128),),
+        in_specs=[pl.BlockSpec(memory_space=pltpu.SMEM)] + [pl.BlockSpec(memory_space=pltpu.HBM)] * 4,
         out_specs=tuple(on_chip(5)),
         scratch_shapes=[
             pltpu.VMEM(cells.shape, jnp.int32),
             pltpu.VMEM(volume.shape, jnp.float32),
-            pltpu.SMEM(live_blocks.shape, jnp.int32),
-            pltpu.SemaphoreType.DMA((10,)),
+            pltpu.SemaphoreType.DMA((9,)),
         ],
         compiler_params=small(),
         name="deposit",
-    )(live_blocks, *(pltpu.with_memory_space_constraint(value, pltpu.HBM) for value in (cells, volume, fluid_velocity, particles)))
-    x_odd = swapped(x_odd, "gx", 1)
-    x_even = swapped(x_even, "gx", 0)
+    )(live_blocks, *fetched)
+    from_odd = swapped(x_odd, "gx", 1)
+    from_even = swapped(x_even, "gx", 0)
     tile, y_up, y_down, flow = pl.pallas_call(
         middle_kernel,
         out_shape=(array_of(tile_rows, 128), array_of(y_rows, 128), array_of(y_rows, 128), array_of(96, 128)),
-        in_specs=on_chip(4),
+        in_specs=on_chip(6),
         out_specs=tuple(on_chip(4)),
         compiler_params=small(),
         name="middle",
-    )(tile, fluid_velocity, x_odd, x_even)
+    )(late, fluid_velocity, x_odd, x_even, from_odd, from_even)
     below_even = one_way(y_up, "gy", 1, 1)
     above_even = one_way(y_down, "gy", 1, -1)
-    early_in = (cells, fluid_velocity, tile, flow)
+    early_in = (cells, share, fluid_velocity, tile, flow)
     sums_even = early(0, early_in)
     below_odd = one_way(y_up, "gy", 0, 1)
     above_odd = one_way(y_down, "gy", 0, -1)
     sums_odd = early(1, early_in)
     rest = (cells, share, particles, tile, y_up, y_down)
-    result = drag_of(0, rest + (below_even, above_even, sums_even), ())
-    void, drag = drag_of(1, rest + (below_odd, above_odd, sums_odd), result)
+    result = drag_of(0, rest + (below_even, above_even, *sums_even), ())
+    void, drag = drag_of(1, rest + (below_odd, above_odd, *sums_odd), result)
     return void, jnp.transpose(drag, (1, 0, 2))[None, None]
 
 

time: 44.9 us -> 45.8 us (1.020)
  Pallas kernels: 8.05 us -> 8.93 us
    pallas_call x3, Pallas kernels: 5.98 us -> 6.84 us  [the longest x2 4.48 us: early(): pl.pallas_call(functools.partial(early_kernel, side), out_shape=(array_of...]
  transfers between devices with their start and end apart: 6 -> 6, of which waited for: 1 -> 1; matrix products, arithmetic and copies ran while one was open for 0% -> 0% of each run, Pallas kernels for 11% -> 14%
where the time goes in v5:
time: 45.8 us; the launch traced here: 45.5 us
  starting transfers between devices  34.2 us (75%)
  Pallas kernels  8.93 us (19%)
  between operations  1.44 us (3%)
  waiting for transfers between devices  0.86 us (2%)
    ppermute x4, starting transfers between devices, one_way(): lax.ppermute(value, axis, [(i, (i + step) % count) for i in range(count)...  20.6 us
    ppermute x2, starting transfers between devices, swapped(): lax.ppermute(value, axis, [(i, (i + 1 if i % 2 == odd else i - 1) % count...  13.6 us
    pallas_call x2, Pallas kernels, early(): pl.pallas_call(functools.partial(early_kernel, side), out_shape=(array_of...  4.48 us
    pallas_call x1, Pallas kernels, body(): pl.pallas_call(deposit_kernel, out_shape=tuple((array_of(rows, 128) for r...  2.36 us
    pallas_call x2, Pallas kernels, drag_of(): pl.pallas_call(functools.partial(drag_kernel, side), out_shape=(array_of(...  2.05 us
  transfers between devices with their start and end apart: 6, of which 1 were waited for; matrix products, arithmetic and copies ran while one was open for 0% of the time, Pallas kernels for 14%

profile of v5, /device:TPU:1, one launch (start us, length us, event | category | flops | bytes accessed | tf_op | source)
XLA Modules:
  0.0 45.5 jit_solution(10360115716602792416)
XLA Ops:
  0.6 0.0 copy-start.1
  1.3 2.4 %deposit.1 = (f32[88,128]{1,0:T(8,128)S(1)}, f32[88,128]{1,0:T(8,128)S(1)}, f32[8,128]{1,0:T(8,128)S(1)}, f32[4,128]{1,0:T(4,128)S(1)}, f32[3,4,128]{2,1,0:T(4,128)S(1)}) custom-call(s32[1,1]{1,0:T(1,128)S(6)} %copy.11.live_ref, s32[29,4,128]{2,1,0:T(4,128)} %bitcast.10, f32[4,128]{1,0:T(4,128)} %bitcast.17, f32[3,4,16,128]{3,2,1,0:T(8,128)} %velocity_ref.7, ...), custom_call_target="tpu_custom_call" | custom-call | tf_op jit(solution)/shard_map/deposit/pallas_call | solution.py:342
  3.7 5.4 %collective-permute-start = (f32[88,128]{1,0:T(8,128)S(1)}, f32[88,128]{1,0:T(8,128)S(1)}, u32[]{:S(2)}, u32[]{:S(2)}) collective-permute-start(f32[88,128]{1,0:T(8,128)S(1)} %get-tuple-element.22.refs_0_), channel_id=1, source_target_pairs={{0,504},{8,16},{16,8},{24,32},{32,24},{40,48},{48,40},{56,64},{64,... | collective-permute-start | bytes 135176 | tf_op jit(solution)/shard_map/ppermute | solution.py:295
  9.1 8.3 %collective-permute-start.1 = (f32[88,128]{1,0:T(8,128)S(1)}, f32[88,128]{1,0:T(8,128)S(1)}, u32[]{:S(2)}, u32[]{:S(2)}) collective-permute-start(f32[88,128]{1,0:T(8,128)S(1)} %get-tuple-element.23.refs_1_), channel_id=1, source_target_pairs={{0,8},{8,0},{16,24},{24,16},{32,40},{40,32},{48,56},{56,48},{64,72... | collective-permute-start | bytes 135176 | tf_op jit(solution)/shard_map/ppermute | solution.py:295
  17.3 0.0 collective-permute-done.refs_2_
  17.4 0.8 %collective-permute-done.1.refs_3_ = f32[88,128]{1,0:T(8,128)S(1)} collective-permute-done((f32[88,128]{1,0:T(8,128)S(1)}, f32[88,128]{1,0:T(8,128)S(1)}, u32[]{:S(2)}, u32[]{:S(2)}) %collective-permute-start.1) | collective-permute-done | bytes 45088 | tf_op jit(solution)/shard_map/ppermute | solution.py:295
  18.2 0.0 copy-done.1
  18.2 0.0 copy-start
  18.2 1.3 %collective-permute-start.4 = (f32[40,128]{1,0:T(8,128)S(1)}, f32[40,128]{1,0:T(8,128)S(1)}, u32[]{:S(2)}, u32[]{:S(2)}) collective-permute-start(f32[40,128]{1,0:T(8,128)S(1)} %get-tuple-element.25.refs_4_), channel_id=1, source_target_pairs={{1,2},{3,4},{5,6},{7,0},{9,10},{11,12},{13,14},{15,8},{17,18},{19,... | collective-permute-start | bytes 61448 | tf_op jit(solution)/shard_map/ppermute | solution.py:300
  19.5 8.8 %collective-permute-start.2 = (f32[40,128]{1,0:T(8,128)S(1)}, f32[40,128]{1,0:T(8,128)S(1)}, u32[]{:S(2)}, u32[]{:S(2)}) collective-permute-start(f32[40,128]{1,0:T(8,128)S(1)} %get-tuple-element.25.refs_4_), channel_id=1, source_target_pairs={{0,1},{2,3},{4,5},{6,7},{8,9},{10,11},{12,13},{14,15},{16,17},{18,... | collective-permute-start | bytes 61448 | tf_op jit(solution)/shard_map/ppermute | solution.py:300
  28.4 1.3 %collective-permute-start.5 = (f32[40,128]{1,0:T(8,128)S(1)}, f32[40,128]{1,0:T(8,128)S(1)}, u32[]{:S(2)}, u32[]{:S(2)}) collective-permute-start(f32[40,128]{1,0:T(8,128)S(1)} %get-tuple-element.26.refs_5_), channel_id=1, source_target_pairs={{1,0},{3,2},{5,4},{7,6},{9,8},{11,10},{13,12},{15,14},{17,16},{19,... | collective-permute-start | bytes 61448 | tf_op jit(solution)/shard_map/ppermute | solution.py:300
  29.7 9.2 %collective-permute-start.3 = (f32[40,128]{1,0:T(8,128)S(1)}, f32[40,128]{1,0:T(8,128)S(1)}, u32[]{:S(2)}, u32[]{:S(2)}) collective-permute-start(f32[40,128]{1,0:T(8,128)S(1)} %get-tuple-element.26.refs_5_), channel_id=1, source_target_pairs={{0,7},{2,1},{4,3},{6,5},{8,15},{10,9},{12,11},{14,13},{16,23},{18,... | collective-permute-start | bytes 61448 | tf_op jit(solution)/shard_map/ppermute | solution.py:300
  38.9 0.0 copy-done
  38.9 4.5 %shard_map.69 = (f32[4,4,128]{2,1,0:T(4,128)S(1)}, f32[32,128]{1,0:T(8,128)S(1)}) custom-call(s32[29,4,128]{2,1,0:T(4,128)S(1)} %bitcast.11, f32[4,128]{1,0:T(4,128)S(1)} %get-tuple-element.19.share_ref.refs_1_, f32[3,4,16,128]{3,2,1,0:T(8,128)S(1)} %copy-done.1, f32[112,128]{1,0:T(8,128)S(1)} %get-tuple-element.24.tile_ref.refs_3_, ...), custom_call_target="tpu_custom_call" | custom-call | flops 3000000000 | bytes 300000 | tf_op jit(solution)/shard_map/pallas_call | solution.py:304
  43.4 0.0 collective-permute-done.4.refs_6_
  43.4 0.0 collective-permute-done.5.refs_7_
  43.4 2.0 %shard_map.70 = (f32[4,16,128]{2,1,0:T(8,128)}, f32[3,4,128]{2,1,0:T(4,128)}) custom-call(s32[29,4,128]{2,1,0:T(4,128)S(1)} %bitcast.13, f32[4,128]{1,0:T(4,128)S(1)} %get-tuple-element.19.share_ref.refs_1_, f32[3,4,128]{2,1,0:T(4,128)S(1)} %get-tuple-element.20.refs_2_, f32[112,128]{1,0:T(8,128)S(1)} %get-tuple-element.24.tile_ref.refs_3_, ...), custom_call_target="tpu_custom_call" | custom-call | tf_op jit(solution)/shard_map/pallas_call | solution.py:317
  45.4 0.0 collective-permute-done.2.refs_6_
  45.4 0.0 collective-permute-done.3.refs_7_
  (3 shorter events, 0.1 us)
Async XLA Ops:
  0.6 17.6 %copy-start.1 = (f32[3,4,16,128]{3,2,1,0:T(8,128)S(1)}, f32[3,4,16,128]{3,2,1,0:T(8,128)}, u32[]{:S(2)}) copy-start(f32[3,4,16,128]{3,2,1,0:T(8,128)} %velocity_ref.7) | copy-start | bytes 294916
  3.7 13.7 %collective-permute-start = (f32[88,128]{1,0:T(8,128)S(1)}, f32[88,128]{1,0:T(8,128)S(1)}, u32[]{:S(2)}, u32[]{:S(2)}) collective-permute-start(f32[88,128]{1,0:T(8,128)S(1)} %get-tuple-element.22.refs_0_), channel_id=1, source_target_pairs={{0,504},{8,16},{16,8},{24,32},{32,24},{40,48},{48,40},{56,64},{64,... | collective-permute-start | bytes 135176 | tf_op jit(solution)/shard_map/ppermute | solution.py:295
  9.1 9.1 %collective-permute-start.1 = (f32[88,128]{1,0:T(8,128)S(1)}, f32[88,128]{1,0:T(8,128)S(1)}, u32[]{:S(2)}, u32[]{:S(2)}) collective-permute-start(f32[88,128]{1,0:T(8,128)S(1)} %get-tuple-element.23.refs_1_), channel_id=1, source_target_pairs={{0,8},{8,0},{16,24},{24,16},{32,40},{40,32},{48,56},{56,48},{64,72... | collective-permute-start | bytes 135176 | tf_op jit(solution)/shard_map/ppermute | solution.py:295
  18.2 20.7 %copy-start = (s32[1,1,4,29,128]{4,2,3,1,0:T(4,128)S(1)}, s32[1,1,4,29,128]{4,2,3,1,0:T(4,128)}, u32[]{:S(2)}) copy-start(s32[1,1,4,29,128]{4,2,3,1,0:T(4,128)} %param.8) | copy-start | bytes 178180
  18.2 25.1 %collective-permute-start.4 = (f32[40,128]{1,0:T(8,128)S(1)}, f32[40,128]{1,0:T(8,128)S(1)}, u32[]{:S(2)}, u32[]{:S(2)}) collective-permute-start(f32[40,128]{1,0:T(8,128)S(1)} %get-tuple-element.25.refs_4_), channel_id=1, source_target_pairs={{1,2},{3,4},{5,6},{7,0},{9,10},{11,12},{13,14},{15,8},{17,18},{19,... | collective-permute-start | bytes 61448 | tf_op jit(solution)/shard_map/ppermute | solution.py:300
  19.5 25.9 %collective-permute-start.2 = (f32[40,128]{1,0:T(8,128)S(1)}, f32[40,128]{1,0:T(8,128)S(1)}, u32[]{:S(2)}, u32[]{:S(2)}) collective-permute-start(f32[40,128]{1,0:T(8,128)S(1)} %get-tuple-element.25.refs_4_), channel_id=1, source_target_pairs={{0,1},{2,3},{4,5},{6,7},{8,9},{10,11},{12,13},{14,15},{16,17},{18,... | collective-permute-start | bytes 61448 | tf_op jit(solution)/shard_map/ppermute | solution.py:300
  28.4 15.0 %collective-permute-start.5 = (f32[40,128]{1,0:T(8,128)S(1)}, f32[40,128]{1,0:T(8,128)S(1)}, u32[]{:S(2)}, u32[]{:S(2)}) collective-permute-start(f32[40,128]{1,0:T(8,128)S(1)} %get-tuple-element.26.refs_5_), channel_id=1, source_target_pairs={{1,0},{3,2},{5,4},{7,6},{9,8},{11,10},{13,12},{15,14},{17,16},{19,... | collective-permute-start | bytes 61448 | tf_op jit(solution)/shard_map/ppermute | solution.py:300
  29.7 15.8 %collective-permute-start.3 = (f32[40,128]{1,0:T(8,128)S(1)}, f32[40,128]{1,0:T(8,128)S(1)}, u32[]{:S(2)}, u32[]{:S(2)}) collective-permute-start(f32[40,128]{1,0:T(8,128)S(1)} %get-tuple-element.26.refs_5_), channel_id=1, source_target_pairs={{0,7},{2,1},{4,3},{6,5},{8,15},{10,9},{12,11},{14,13},{16,23},{18,... | collective-permute-start | bytes 61448 | tf_op jit(solution)/shard_map/ppermute | solution.py:300

commit v6 on v5

--- a/solution.py
+++ b/solution.py
@@ -261,6 +261,8 @@
             void_ref[i - 1, 0:1] = late_void[wide_x + i : wide_x + i + 1]
             void_ref[i - 1, 1 : 1 + own_y] = early_void[i * own_y : (i + 1) * own_y]
             void_ref[i - 1, 1 + own_y : 2 + own_y] = late_void[2 * wide_x + i : 2 * wide_x + i + 1]
+        void_copy = pltpu.make_async_copy(void_ref, void_out, sems.at[0])
+        void_copy.start()
         resistance = resistance_of(late_void)
         fields = [resistance]
         for f in range(3):
@@ -272,14 +274,10 @@
             for f in range(3):
                 force = total[f + 1] - particle_ref[f, b : b + 1] * total[0]
                 drag_ref[f, b : b + 1] = drag_scale * share_ref[b : b + 1] * force
-        copies = [
-            pltpu.make_async_copy(void_ref, void_out, sems.at[0]),
-            pltpu.make_async_copy(drag_ref, drag_out, sems.at[1]),
-        ]
-        for copy in copies:
-            copy.start()
-        for copy in copies:
-            copy.wait()
+        drag_copy = pltpu.make_async_copy(drag_ref, drag_out, sems.at[1])
+        drag_copy.start()
+        drag_copy.wait()
+        void_copy.wait()
 
 
 def on_chip(count):

time: 45.8 us -> 45.8 us (level)
  no operation moved by 1% of the time
where the time goes in v6:
time: 45.8 us; the launch traced here: 45.5 us
  starting transfers between devices  34.2 us (75%)
  Pallas kernels  8.93 us (19%)
  between operations  1.44 us (3%)
  waiting for transfers between devices  0.86 us (2%)
    ppermute x4, starting transfers between devices, one_way(): lax.ppermute(value, axis, [(i, (i + step) % count) for i in range(count)...  20.6 us
    ppermute x2, starting transfers between devices, swapped(): lax.ppermute(value, axis, [(i, (i + 1 if i % 2 == odd else i - 1) % count...  13.6 us
    pallas_call x2, Pallas kernels, early(): pl.pallas_call(functools.partial(early_kernel, side), out_shape=(array_of...  4.48 us
    pallas_call x1, Pallas kernels, body(): pl.pallas_call(deposit_kernel, out_shape=tuple((array_of(rows, 128) for r...  2.36 us
    pallas_call x2, Pallas kernels, drag_of(): pl.pallas_call(functools.partial(drag_kernel, side), out_shape=(array_of(...  2.05 us
  transfers between devices with their start and end apart: 6, of which 1 were waited for; matrix products, arithmetic and copies ran while one was open for 0% of the time, Pallas kernels for 14%

profile of v6, /device:TPU:1, one launch (start us, length us, event | category | flops | bytes accessed | tf_op | source)
XLA Modules:
  0.0 45.5 jit_solution(16061365397463516958)
XLA Ops:
  0.6 0.0 copy-start.1
  1.3 2.4 %deposit.1 = (f32[88,128]{1,0:T(8,128)S(1)}, f32[88,128]{1,0:T(8,128)S(1)}, f32[8,128]{1,0:T(8,128)S(1)}, f32[4,128]{1,0:T(4,128)S(1)}, f32[3,4,128]{2,1,0:T(4,128)S(1)}) custom-call(s32[1,1]{1,0:T(1,128)S(6)} %copy.11.live_ref, s32[29,4,128]{2,1,0:T(4,128)} %bitcast.10, f32[4,128]{1,0:T(4,128)} %bitcast.17, f32[3,4,16,128]{3,2,1,0:T(8,128)} %velocity_ref.7, ...), custom_call_target="tpu_custom_call" | custom-call | tf_op jit(solution)/shard_map/deposit/pallas_call | solution.py:340
  3.7 5.4 %collective-permute-start = (f32[88,128]{1,0:T(8,128)S(1)}, f32[88,128]{1,0:T(8,128)S(1)}, u32[]{:S(2)}, u32[]{:S(2)}) collective-permute-start(f32[88,128]{1,0:T(8,128)S(1)} %get-tuple-element.22.refs_0_), channel_id=1, source_target_pairs={{0,504},{8,16},{16,8},{24,32},{32,24},{40,48},{48,40},{56,64},{64,... | collective-permute-start | bytes 135176 | tf_op jit(solution)/shard_map/ppermute | solution.py:293
  9.1 8.3 %collective-permute-start.1 = (f32[88,128]{1,0:T(8,128)S(1)}, f32[88,128]{1,0:T(8,128)S(1)}, u32[]{:S(2)}, u32[]{:S(2)}) collective-permute-start(f32[88,128]{1,0:T(8,128)S(1)} %get-tuple-element.23.refs_1_), channel_id=1, source_target_pairs={{0,8},{8,0},{16,24},{24,16},{32,40},{40,32},{48,56},{56,48},{64,72... | collective-permute-start | bytes 135176 | tf_op jit(solution)/shard_map/ppermute | solution.py:293
  17.3 0.0 collective-permute-done.refs_2_
  17.4 0.8 %collective-permute-done.1.refs_3_ = f32[88,128]{1,0:T(8,128)S(1)} collective-permute-done((f32[88,128]{1,0:T(8,128)S(1)}, f32[88,128]{1,0:T(8,128)S(1)}, u32[]{:S(2)}, u32[]{:S(2)}) %collective-permute-start.1) | collective-permute-done | bytes 45088 | tf_op jit(solution)/shard_map/ppermute | solution.py:293
  18.2 0.0 copy-done.1
  18.2 0.0 copy-start
  18.2 1.3 %collective-permute-start.4 = (f32[40,128]{1,0:T(8,128)S(1)}, f32[40,128]{1,0:T(8,128)S(1)}, u32[]{:S(2)}, u32[]{:S(2)}) collective-permute-start(f32[40,128]{1,0:T(8,128)S(1)} %get-tuple-element.25.refs_4_), channel_id=1, source_target_pairs={{1,2},{3,4},{5,6},{7,0},{9,10},{11,12},{13,14},{15,8},{17,18},{19,... | collective-permute-start | bytes 61448 | tf_op jit(solution)/shard_map/ppermute | solution.py:298
  19.5 8.8 %collective-permute-start.2 = (f32[40,128]{1,0:T(8,128)S(1)}, f32[40,128]{1,0:T(8,128)S(1)}, u32[]{:S(2)}, u32[]{:S(2)}) collective-permute-start(f32[40,128]{1,0:T(8,128)S(1)} %get-tuple-element.25.refs_4_), channel_id=1, source_target_pairs={{0,1},{2,3},{4,5},{6,7},{8,9},{10,11},{12,13},{14,15},{16,17},{18,... | collective-permute-start | bytes 61448 | tf_op jit(solution)/shard_map/ppermute | solution.py:298
  28.4 1.3 %collective-permute-start.5 = (f32[40,128]{1,0:T(8,128)S(1)}, f32[40,128]{1,0:T(8,128)S(1)}, u32[]{:S(2)}, u32[]{:S(2)}) collective-permute-start(f32[40,128]{1,0:T(8,128)S(1)} %get-tuple-element.26.refs_5_), channel_id=1, source_target_pairs={{1,0},{3,2},{5,4},{7,6},{9,8},{11,10},{13,12},{15,14},{17,16},{19,... | collective-permute-start | bytes 61448 | tf_op jit(solution)/shard_map/ppermute | solution.py:298
  29.7 9.2 %collective-permute-start.3 = (f32[40,128]{1,0:T(8,128)S(1)}, f32[40,128]{1,0:T(8,128)S(1)}, u32[]{:S(2)}, u32[]{:S(2)}) collective-permute-start(f32[40,128]{1,0:T(8,128)S(1)} %get-tuple-element.26.refs_5_), channel_id=1, source_target_pairs={{0,7},{2,1},{4,3},{6,5},{8,15},{10,9},{12,11},{14,13},{16,23},{18,... | collective-permute-start | bytes 61448 | tf_op jit(solution)/shard_map/ppermute | solution.py:298
  38.9 0.0 copy-done
  38.9 4.5 %shard_map.69 = (f32[4,4,128]{2,1,0:T(4,128)S(1)}, f32[32,128]{1,0:T(8,128)S(1)}) custom-call(s32[29,4,128]{2,1,0:T(4,128)S(1)} %bitcast.11, f32[4,128]{1,0:T(4,128)S(1)} %get-tuple-element.19.share_ref.refs_1_, f32[3,4,16,128]{3,2,1,0:T(8,128)S(1)} %copy-done.1, f32[112,128]{1,0:T(8,128)S(1)} %get-tuple-element.24.tile_ref.refs_3_, ...), custom_call_target="tpu_custom_call" | custom-call | flops 3000000000 | bytes 300000 | tf_op jit(solution)/shard_map/pallas_call | solution.py:302
  43.4 0.0 collective-permute-done.4.refs_6_
  43.4 0.0 collective-permute-done.5.refs_7_
  43.4 2.0 %shard_map.70 = (f32[4,16,128]{2,1,0:T(8,128)}, f32[3,4,128]{2,1,0:T(4,128)}) custom-call(s32[29,4,128]{2,1,0:T(4,128)S(1)} %bitcast.13, f32[4,128]{1,0:T(4,128)S(1)} %get-tuple-element.19.share_ref.refs_1_, f32[3,4,128]{2,1,0:T(4,128)S(1)} %get-tuple-element.20.refs_2_, f32[112,128]{1,0:T(8,128)S(1)} %get-tuple-element.24.tile_ref.refs_3_, ...), custom_call_target="tpu_custom_call" | custom-call | tf_op jit(solution)/shard_map/pallas_call | solution.py:315
  45.4 0.0 collective-permute-done.2.refs_6_
  45.4 0.0 collective-permute-done.3.refs_7_
  (3 shorter events, 0.1 us)
Async XLA Ops:
  0.6 17.6 %copy-start.1 = (f32[3,4,16,128]{3,2,1,0:T(8,128)S(1)}, f32[3,4,16,128]{3,2,1,0:T(8,128)}, u32[]{:S(2)}) copy-start(f32[3,4,16,128]{3,2,1,0:T(8,128)} %velocity_ref.7) | copy-start | bytes 294916
  3.7 13.7 %collective-permute-start = (f32[88,128]{1,0:T(8,128)S(1)}, f32[88,128]{1,0:T(8,128)S(1)}, u32[]{:S(2)}, u32[]{:S(2)}) collective-permute-start(f32[88,128]{1,0:T(8,128)S(1)} %get-tuple-element.22.refs_0_), channel_id=1, source_target_pairs={{0,504},{8,16},{16,8},{24,32},{32,24},{40,48},{48,40},{56,64},{64,... | collective-permute-start | bytes 135176 | tf_op jit(solution)/shard_map/ppermute | solution.py:293
  9.1 9.1 %collective-permute-start.1 = (f32[88,128]{1,0:T(8,128)S(1)}, f32[88,128]{1,0:T(8,128)S(1)}, u32[]{:S(2)}, u32[]{:S(2)}) collective-permute-start(f32[88,128]{1,0:T(8,128)S(1)} %get-tuple-element.23.refs_1_), channel_id=1, source_target_pairs={{0,8},{8,0},{16,24},{24,16},{32,40},{40,32},{48,56},{56,48},{64,72... | collective-permute-start | bytes 135176 | tf_op jit(solution)/shard_map/ppermute | solution.py:293
  18.2 20.7 %copy-start = (s32[1,1,4,29,128]{4,2,3,1,0:T(4,128)S(1)}, s32[1,1,4,29,128]{4,2,3,1,0:T(4,128)}, u32[]{:S(2)}) copy-start(s32[1,1,4,29,128]{4,2,3,1,0:T(4,128)} %param.8) | copy-start | bytes 178180
  18.2 25.1 %collective-permute-start.4 = (f32[40,128]{1,0:T(8,128)S(1)}, f32[40,128]{1,0:T(8,128)S(1)}, u32[]{:S(2)}, u32[]{:S(2)}) collective-permute-start(f32[40,128]{1,0:T(8,128)S(1)} %get-tuple-element.25.refs_4_), channel_id=1, source_target_pairs={{1,2},{3,4},{5,6},{7,0},{9,10},{11,12},{13,14},{15,8},{17,18},{19,... | collective-permute-start | bytes 61448 | tf_op jit(solution)/shard_map/ppermute | solution.py:298
  19.5 25.9 %collective-permute-start.2 = (f32[40,128]{1,0:T(8,128)S(1)}, f32[40,128]{1,0:T(8,128)S(1)}, u32[]{:S(2)}, u32[]{:S(2)}) collective-permute-start(f32[40,128]{1,0:T(8,128)S(1)} %get-tuple-element.25.refs_4_), channel_id=1, source_target_pairs={{0,1},{2,3},{4,5},{6,7},{8,9},{10,11},{12,13},{14,15},{16,17},{18,... | collective-permute-start | bytes 61448 | tf_op jit(solution)/shard_map/ppermute | solution.py:298
  28.4 15.0 %collective-permute-start.5 = (f32[40,128]{1,0:T(8,128)S(1)}, f32[40,128]{1,0:T(8,128)S(1)}, u32[]{:S(2)}, u32[]{:S(2)}) collective-permute-start(f32[40,128]{1,0:T(8,128)S(1)} %get-tuple-element.26.refs_5_), channel_id=1, source_target_pairs={{1,0},{3,2},{5,4},{7,6},{9,8},{11,10},{13,12},{15,14},{17,16},{19,... | collective-permute-start | bytes 61448 | tf_op jit(solution)/shard_map/ppermute | solution.py:298
  29.7 15.8 %collective-permute-start.3 = (f32[40,128]{1,0:T(8,128)S(1)}, f32[40,128]{1,0:T(8,128)S(1)}, u32[]{:S(2)}, u32[]{:S(2)}) collective-permute-start(f32[40,128]{1,0:T(8,128)S(1)} %get-tuple-element.26.refs_5_), channel_id=1, source_target_pairs={{0,7},{2,1},{4,3},{6,5},{8,15},{10,9},{12,11},{14,13},{16,23},{18,... | collective-permute-start | bytes 61448 | tf_op jit(solution)/shard_map/ppermute | solution.py:298
